TPU v7x, 512 devices: a whole 4x4x16 slice. The times are simulated.
512 devices in a mesh: cells: 32 (over x, y, core), vocab: 16 (over z).
Axes of the slice: x: 4, y: 4, z: 16, core: 2. Of those that a mesh axis runs over, the one named last changes fastest.
Arguments:
- clean_resid: float32 [32, 2048], P('cells'), may hold values from -130 to 130
- path_delta: bfloat16 [32, 4, 16, 2048], P('cells'), may hold values from -6 to 6
- layer_index: int32 [4064], P('cells'), may hold values from 0 to 3
- pos_index: int32 [4064], P('cells'), may hold values from 0 to 15
- answer_ids: int32 [32], P('cells'), may hold values from 0 to 51199
- norm_gain: float32 [2048], replicated, may hold values from 0.1 to 1.9
- unembed: bfloat16 [2048, 51200], P('cells', 'vocab'), may hold values from -1.5 to 1.5
Outputs:
- divergence: float32 [4064], P('cells')
- answer_logprob: float32 [4064], P('cells')
- total_kl: float32 [], replicated
All inputs are finite; a program needn't handle non-finite values.
Results may differ from a plain program's by a relative error of at most 0.0091.
Values may be sent and summed in bfloat16 or wider, within the bound.
No kernel may reach another device: no remote copies, remote signals or barrier semaphores. Data moves between devices by JAX's collectives and lax.ppermute only.
A program may use at most 64 MiB of HBM per device.

v0:
```python
import functools

import jax
import jax.numpy as jnp
from jax import lax
from jax.experimental import pallas as pl
from jax.experimental.pallas import tpu as pltpu
from jax.sharding import PartitionSpec as P


XS, YS, CORES = 4, 4, 2
SUBS = YS * CORES
PLANE = XS * SUBS
LANES = 128
KEYS = 64
ROWS = 72
FULL = 3
LEFT = LANES // SUBS
NEG = -1e30
F32 = jnp.float32
BF16 = jnp.bfloat16
MIB = 1 << 20
VMEM = pl.BlockSpec(memory_space=pltpu.VMEM)
SMEM = pl.BlockSpec(memory_space=pltpu.SMEM)


def lanes_of(shape):
    return lax.broadcasted_iota(jnp.int32, shape, len(shape) - 1)


def pack_kernel(u_ref, out_ref):
    depth = u_ref.shape[0]
    groups = depth // 8
    last = u_ref[:, SUBS * FULL * LANES :].astype(F32)
    lane = lanes_of((8, LANES))
    for sub in range(SUBS):
        left = jnp.zeros((8, LANES), F32)
        for a in range(groups):
            piece = pltpu.roll(last[8 * a : 8 * a + 8], (LEFT * (a - sub)) % LANES, 1)
            left = jnp.where(lane // LEFT == a, piece, left)
        left = left.astype(BF16)
        for x in range(XS):
            to = x * SUBS + sub
            for k in range(FULL):
                at = (sub * FULL + k) * LANES
                out_ref[to, k * depth : (k + 1) * depth, :] = u_ref[:, at : at + LANES]
            out_ref[to, FULL * depth :, :] = left


def packed(unembed):
    depth = unembed.shape[0]
    return pl.pallas_call(
        pack_kernel,
        out_shape=jax.ShapeDtypeStruct((PLANE, FULL * depth + 8, LANES), BF16),
        in_specs=[VMEM],
        out_specs=VMEM,
        compiler_params=pltpu.CompilerParams(vmem_limit_bytes=8 * MIB),
        name="pack",
    )(unembed)


def key_hits(layer_ref, pos_ref, position_count):
    flat = layer_ref[...] * position_count + pos_ref[...]
    key = lax.broadcasted_iota(jnp.int32, (LANES, flat.shape[1]), 0)
    return (key == flat).astype(F32)


def as_line(column):
    square = (LANES, LANES)
    eye = lax.broadcasted_iota(jnp.int32, square, 0) == lanes_of(square)
    return jnp.sum(jnp.where(eye, column, 0.0), axis=0, keepdims=True)


def norm_kernel(answer_ref, clean_ref, delta_ref, gain_ref, act_ref):
    features = clean_ref.shape[1]
    clean = clean_ref[...]
    gain = gain_ref[...]

    def normed(values):
        mean_square = jnp.sum(values * values, axis=-1, keepdims=True) * (1.0 / features)
        return values * lax.rsqrt(mean_square + 1e-06) * gain

    patched = normed(clean + delta_ref[...].astype(F32)).astype(BF16)
    answer = answer_ref[0]
    high = lax.shift_right_logical(answer, 8).astype(F32)
    low = (answer & 255).astype(F32)
    shape = (ROWS - KEYS, features)
    row = lax.broadcasted_iota(jnp.int32, shape, 0)
    lane = lanes_of(shape)
    digits = jnp.where(lane == 0, high, jnp.where(lane == 1, low, 0.0))
    tail = jnp.where(row == 0, normed(clean), jnp.where(row == 1, digits, 0.0)).astype(BF16)
    act_ref[:KEYS, :] = patched
    act_ref[KEYS:, :] = tail


def normed_rows(answer_ids, clean_resid, delta_table, norm_gain):
    features = clean_resid.shape[1]
    return pl.pallas_call(
        norm_kernel,
        out_shape=jax.ShapeDtypeStruct((ROWS, features), BF16),
        in_specs=[SMEM, VMEM, VMEM, VMEM],
        out_specs=VMEM,
        compiler_params=pltpu.CompilerParams(vmem_limit_bytes=8 * MIB),
        name="norm",
    )(answer_ids, clean_resid, delta_table, norm_gain)


def score_kernel(*refs):
    acts, (w_ref, out_ref, a_buf, w_buf, l_buf) = refs[:SUBS], refs[SUBS:]
    depth = (w_ref.shape[1] - 8) // FULL
    groups = depth // 8
    copies = out_ref.shape[0]
    me = lax.axis_index("cells")
    sub = me % SUBS
    start = lax.axis_index("vocab") * (SUBS * (FULL * LANES + LEFT))
    for i in range(PLANE):
        rows = slice(i * depth, (i + 1) * depth)
        for k in range(FULL):
            w_buf[rows, k * LANES : (k + 1) * LANES] = w_ref[i, k * depth : (k + 1) * depth, :]
        left = w_ref[i, FULL * depth :, :].astype(F32)
        pieces = [left] + [pltpu.roll(left, LANES - LEFT * a, 1) for a in range(1, groups)]
        w_buf[rows, FULL * LANES :] = jnp.concatenate(pieces, axis=0).astype(BF16)
    for j in range(SUBS):
        a_buf[j * ROWS : (j + 1) * ROWS, :] = acts[j][...]
    l_buf[...] = jnp.dot(a_buf[...], w_buf[...], preferred_element_type=F32)

    width = (FULL + 1) * LANES
    lane = lanes_of((1, width))
    kept = lane < FULL * LANES + LEFT
    column = jnp.where(
        lane < FULL * LANES,
        start + sub * (FULL * LANES) + lane,
        start + SUBS * FULL * LANES + sub * LEFT + lane - FULL * LANES,
    ).astype(F32)
    for t in range(YS):
        parts = []
        for d in range(CORES):
            at = (d * YS + t) * ROWS
            clean = jnp.where(kept, l_buf[at + KEYS : at + KEYS + 1, :], NEG)
            max_clean = jnp.max(clean, axis=-1, keepdims=True)
            weight = jnp.exp(clean - max_clean)
            sum_clean = jnp.sum(weight, axis=-1, keepdims=True)
            weight = weight * (1.0 / sum_clean)
            clean_lse = max_clean + jnp.log(sum_clean)
            tail = acts[d * YS + t][KEYS:, 0:LANES].astype(F32)
            digits = tail[1:2]
            answer = digits[:, 0:1] * 256.0 + digits[:, 1:2]
            logits = jnp.where(kept, l_buf[at : at + KEYS, :], NEG)
            max_patch = jnp.max(logits, axis=-1, keepdims=True)
            sum_patch = jnp.sum(jnp.exp(logits - max_patch), axis=-1, keepdims=True)
            cross = jnp.sum(weight * (clean - logits), axis=-1, keepdims=True)
            picked = jnp.where((column == answer) & kept, logits, 0.0)
            parts.append(
                (
                    max_patch + jnp.log(sum_patch),
                    cross,
                    jnp.sum(picked, axis=-1, keepdims=True),
                    jnp.broadcast_to(clean_lse, (KEYS, 1)),
                )
            )
        for k in range(4):
            both = jnp.concatenate([parts[0][k], parts[1][k]], axis=0)
            line = as_line(both)
            for i in range(copies):
                out_ref[i, 4 * k + t : 4 * k + t + 1, :] = line


def scored(acts, weights, copies):
    depth = (weights.shape[1] - 8) // FULL
    return pl.pallas_call(
        score_kernel,
        out_shape=jax.ShapeDtypeStruct((copies, 16, LANES), F32),
        in_specs=[VMEM] * (SUBS + 1),
        out_specs=VMEM,
        scratch_shapes=[
            pltpu.VMEM((SUBS * ROWS, acts[0].shape[1]), BF16),
            pltpu.VMEM((PLANE * depth, (FULL + 1) * LANES), BF16),
            pltpu.VMEM((2 * YS * ROWS, (FULL + 1) * LANES), F32),
        ],
        compiler_params=pltpu.CompilerParams(vmem_limit_bytes=24 * MIB),
        name="score",
    )(*acts, weights)


def merged(lse, cross, answer, clean_lse):
    top = jnp.max(lse, axis=0)
    lse = top + jnp.log(jnp.sum(jnp.exp(lse - top), axis=0))
    top = jnp.max(clean_lse, axis=0)
    weight = jnp.exp(clean_lse - top)
    total = jnp.sum(weight, axis=0)
    cross = jnp.sum(weight * cross, axis=0) / total
    return lse, cross, jnp.sum(answer, axis=0), top + jnp.log(total)


def merge_kernel(in_ref, layer_ref, pos_ref, out_ref, *, position_count):
    me = lax.axis_index("cells")
    y, core = (me // CORES) % YS, me % CORES
    lines = []
    for value in merged(*(in_ref[:, 4 * k : 4 * k + 4, :] for k in range(4))):
        value = jnp.where(core == 1, pltpu.roll(value, KEYS, 1), value)
        placed = value
        for shift in range(1, YS):
            turned = jnp.concatenate([value[YS - shift :], value[: YS - shift]], axis=0)
            placed = jnp.where(y == shift, turned, placed)
        lines.append(placed)
    hits = key_hits(layer_ref, pos_ref, position_count)
    count = as_line(jnp.sum(hits, axis=1, keepdims=True))
    lane = lanes_of((YS, LANES))
    row = lax.broadcasted_iota(jnp.int32, (YS, LANES), 0)
    half = KEYS // 2
    count = jnp.where(row == 0, pltpu.roll(count, half, 1), count)
    lines[3] = jnp.where((lane // half == 1) & (row < 2), count, lines[3])
    for i in range(out_ref.shape[0]):
        for k in range(4):
            out_ref[i, 4 * k : 4 * k + 4, :] = lines[k]


def merged_over_vocab(pieces, layer, pos, position_count):
    return pl.pallas_call(
        functools.partial(merge_kernel, position_count=position_count),
        out_shape=jax.ShapeDtypeStruct((PLANE, 16, LANES), F32),
        in_specs=[VMEM, VMEM, VMEM],
        out_specs=VMEM,
        compiler_params=pltpu.CompilerParams(vmem_limit_bytes=8 * MIB),
        name="merge",
    )(pieces, layer, pos)


def finish_kernel(in_ref, layer_ref, pos_ref, div_ref, log_ref, total_ref, *, position_count):
    me = lax.axis_index("cells")
    shape = (YS, LANES)
    row = lax.broadcasted_iota(jnp.int32, shape, 0)
    lane = lanes_of(shape)
    half = KEYS // 2
    own_row = (me // CORES) % YS
    total = jnp.zeros(shape, F32)
    own_div = jnp.zeros(shape, F32)
    own_log = jnp.zeros(shape, F32)
    for x in range(XS):
        group = slice(x * SUBS, (x + 1) * SUBS)
        clean = in_ref[group, 12:16, :]
        spread = [
            jnp.where(lane % KEYS < half, clean[s], pltpu.roll(clean[s], half, 1))[None]
            for s in range(SUBS)
        ]
        lse, cross, answer, clean_lse = merged(
            *(in_ref[group, 4 * k : 4 * k + 4, :] for k in range(3)),
            jnp.concatenate(spread, axis=0),
        )
        divergence = cross - clean_lse + lse
        for s in range(SUBS):
            y, core = s // CORES, s % CORES
            left = pltpu.roll(clean[s], (core * KEYS - half) % LANES, 1)[0:1]
            right = clean[s][1:2]
            if core == 1:
                right = pltpu.roll(clean[s], KEYS, 1)[1:2]
            count = jnp.where(lane[0:1] % KEYS < half, left, right)
            count = jnp.where(lane[0:1] // KEYS == core, count, 0.0)
            total = total + jnp.where(row == y, count * divergence, 0.0)
        mine = (row == own_row) & (me // SUBS == x)
        own_div = jnp.where(mine, divergence, own_div)
        own_log = jnp.where(mine, answer - lse, own_log)
    total_ref[...] = jnp.sum(jnp.sum(total, axis=0, keepdims=True), axis=1, keepdims=True)
    own = jnp.concatenate(
        [
            jnp.sum(own_div, axis=0, keepdims=True),
            jnp.sum(own_log, axis=0, keepdims=True),
            jnp.zeros((6, LANES), F32),
        ],
        axis=0,
    )
    own = jnp.where(me % CORES == 1, pltpu.roll(own, KEYS, 1), own)
    hits = key_hits(layer_ref, pos_ref, position_count)
    out = jnp.dot(own, hits, preferred_element_type=F32, precision=lax.Precision.HIGHEST)
    div_ref[...] = out[0]
    log_ref[...] = out[1]


def finished(pieces, layer, pos, position_count):
    cells = layer.shape[1]
    return pl.pallas_call(
        functools.partial(finish_kernel, position_count=position_count),
        out_shape=(
            jax.ShapeDtypeStruct((cells,), F32),
            jax.ShapeDtypeStruct((cells,), F32),
            jax.ShapeDtypeStruct((1, 1), F32),
        ),
        in_specs=[VMEM, VMEM, VMEM],
        out_specs=(VMEM, VMEM, VMEM),
        compiler_params=pltpu.CompilerParams(vmem_limit_bytes=8 * MIB),
        name="finish",
    )(pieces, layer, pos)


def moved(value, to):
    return lax.ppermute(value, "cells", [(i, to(i)) for i in range(PLANE)])


def along_y(step):
    def to(i):
        x, y, core = i // SUBS, (i // CORES) % YS, i % CORES
        return x * SUBS + ((y - step) % YS) * CORES + core

    return to


def on_device(clean_resid, path_delta, layer_index, pos_index, answer_ids, norm_gain, unembed):
    position_count = path_delta.shape[2]
    features = clean_resid.shape[1]
    act = normed_rows(
        answer_ids,
        clean_resid,
        path_delta.reshape(KEYS, features),
        norm_gain.reshape(1, features),
    )
    same = [act]
    for step in range(1, YS):
        same.append(moved(act, along_y(step)))
    weights = lax.all_to_all(packed(unembed), "cells", 0, 0, tiled=True)
    other = []
    for step in range(YS):
        other.append(moved(same[step], lambda i: i ^ 1))
    stats = scored(same + other, weights, lax.axis_size("vocab"))
    stats = lax.all_to_all(stats, "vocab", 0, 0, tiled=True)
    layer, pos = layer_index.reshape(1, -1), pos_index.reshape(1, -1)
    pieces = merged_over_vocab(stats, layer, pos, position_count)
    pieces = lax.all_to_all(pieces, "cells", 0, 0, tiled=True)
    divergence, answer_logprob, total = finished(pieces, layer, pos, position_count)
    return divergence, answer_logprob, total.reshape(())


def solution(mesh):
    in_specs = (
        P("cells", None),
        P("cells", None, None, None),
        P("cells"),
        P("cells"),
        P("cells"),
        P(),
        P("cells", "vocab"),
    )
    out_specs = (P("cells"), P("cells"), P())
    return jax.shard_map(
        on_device, mesh=mesh, in_specs=in_specs, out_specs=out_specs, check_vma=False
    )
```

profile of v0, /device:TPU:1, one launch (start us, length us, event | category | flops | bytes accessed | tf_op | source)
XLA Modules:
  0.0 101.6 jit_solution(13034236507420422728)
XLA Ops:
  0.6 1.0 copy-done
  1.6 1.4 %pack.1 = bf16[32,200,128]{2,1,0:T(8,128)(2,1)} custom-call(bf16[64,3200]{1,0:T(8,128)(2,1)S(1)} %copy-done), custom_call_target="tpu_custom_call" | custom-call | tf_op jit(solution)/shard_map/pack/pallas_call | solution.py:52
  3.0 10.6 %all-to-all-start = ((bf16[32,200,128]{2,1,0:T(8,128)(2,1)}), bf16[32,200,128]{2,1,0:T(8,128)(2,1)S(1)}, u32[]{:S(2)}, u32[]{:S(2)}) async-start(bf16[32,200,128]{2,1,0:T(8,128)(2,1)} %pack.1), calls=%async_computation | async-start | bytes 3276800 | tf_op jit(solution)/shard_map/all_to_all | solution.py:319
  14.3 0.0 copy-start.8
  14.3 0.2 norm.1.refs_0_
  14.5 3.3 %collective-permute-start.2 = (bf16[72,2048]{1,0:T(8,128)(2,1)S(1)}, bf16[72,2048]{1,0:T(8,128)(2,1)S(1)}, u32[]{:S(2)}, u32[]{:S(2)}) collective-permute-start(bf16[72,2048]{1,0:T(8,128)(2,1)S(1)} %norm.1.refs_0_), channel_id=1, source_target_pairs={{0,32},{16,48},{32,64},{48,80},{64,96},{80,112},{96,0},{112,16},{1... | collective-permute-start | bytes 884744 | tf_op jit(solution)/shard_map/ppermute | solution.py:296
  17.8 4.3 %collective-permute-start.1 = (bf16[72,2048]{1,0:T(8,128)(2,1)S(1)}, bf16[72,2048]{1,0:T(8,128)(2,1)S(1)}, u32[]{:S(2)}, u32[]{:S(2)}) collective-permute-start(bf16[72,2048]{1,0:T(8,128)(2,1)S(1)} %norm.1.refs_0_), channel_id=1, source_target_pairs={{0,64},{16,80},{32,96},{48,112},{64,0},{80,16},{96,32},{112,48},{1... | collective-permute-start | bytes 884744 | tf_op jit(solution)/shard_map/ppermute | solution.py:296
  22.1 3.1 %collective-permute-start = (bf16[72,2048]{1,0:T(8,128)(2,1)S(1)}, bf16[72,2048]{1,0:T(8,128)(2,1)S(1)}, u32[]{:S(2)}, u32[]{:S(2)}) collective-permute-start(bf16[72,2048]{1,0:T(8,128)(2,1)S(1)} %norm.1.refs_0_), channel_id=1, source_target_pairs={{0,96},{16,112},{32,0},{48,16},{64,32},{80,48},{96,64},{112,80},{1... | collective-permute-start | bytes 884744 | tf_op jit(solution)/shard_map/ppermute | solution.py:296
  25.2 3.1 %collective-permute-start.3 = (bf16[72,2048]{1,0:T(8,128)(2,1)S(1)}, bf16[72,2048]{1,0:T(8,128)(2,1)S(1)}, u32[]{:S(2)}, u32[]{:S(2)}) collective-permute-start(bf16[72,2048]{1,0:T(8,128)(2,1)S(1)} %norm.1.refs_0_), channel_id=1, source_target_pairs={{0,16},{16,0},{32,48},{48,32},{64,80},{80,64},{96,112},{112,96},{1... | collective-permute-start | bytes 884744 | tf_op jit(solution)/shard_map/ppermute | solution.py:296
  28.4 12.5 %collective-permute-done.2.refs_3_ = bf16[72,2048]{1,0:T(8,128)(2,1)S(1)} collective-permute-done((bf16[72,2048]{1,0:T(8,128)(2,1)S(1)}, bf16[72,2048]{1,0:T(8,128)(2,1)S(1)}, u32[]{:S(2)}, u32[]{:S(2)}) %collective-permute-start.2) | collective-permute-done | bytes 294944 | tf_op jit(solution)/shard_map/ppermute | solution.py:296
  40.9 3.1 %collective-permute-start.6 = (bf16[72,2048]{1,0:T(8,128)(2,1)S(1)}, bf16[72,2048]{1,0:T(8,128)(2,1)S(1)}, u32[]{:S(2)}, u32[]{:S(2)}) collective-permute-start(bf16[72,2048]{1,0:T(8,128)(2,1)S(1)} %collective-permute-done.2.refs_3_), channel_id=1, source_target_pairs={{0,16},{16,0},{32,48},{48,32},{64,80},{80,64},{96,112},{112,96},{1... | collective-permute-start | bytes 884744 | tf_op jit(solution)/shard_map/ppermute | solution.py:296
  44.0 3.5 %collective-permute-done.1.refs_2_ = bf16[72,2048]{1,0:T(8,128)(2,1)S(1)} collective-permute-done((bf16[72,2048]{1,0:T(8,128)(2,1)S(1)}, bf16[72,2048]{1,0:T(8,128)(2,1)S(1)}, u32[]{:S(2)}, u32[]{:S(2)}) %collective-permute-start.1) | collective-permute-done | bytes 294944 | tf_op jit(solution)/shard_map/ppermute | solution.py:296
  47.5 2.9 %collective-permute-start.5 = (bf16[72,2048]{1,0:T(8,128)(2,1)S(1)}, bf16[72,2048]{1,0:T(8,128)(2,1)S(1)}, u32[]{:S(2)}, u32[]{:S(2)}) collective-permute-start(bf16[72,2048]{1,0:T(8,128)(2,1)S(1)} %collective-permute-done.1.refs_2_), channel_id=1, source_target_pairs={{0,16},{16,0},{32,48},{48,32},{64,80},{80,64},{96,112},{112,96},{1... | collective-permute-start | bytes 884744 | tf_op jit(solution)/shard_map/ppermute | solution.py:296
  50.4 1.9 %collective-permute-start.4 = (bf16[72,2048]{1,0:T(8,128)(2,1)S(1)}, bf16[72,2048]{1,0:T(8,128)(2,1)S(1)}, u32[]{:S(2)}, u32[]{:S(2)}) collective-permute-start(bf16[72,2048]{1,0:T(8,128)(2,1)S(1)} %collective-permute-done.refs_1_), channel_id=1, source_target_pairs={{0,16},{16,0},{32,48},{48,32},{64,80},{80,64},{96,112},{112,96},{1... | collective-permute-start | bytes 884744 | tf_op jit(solution)/shard_map/ppermute | solution.py:296
  52.4 0.7 copy-done.1
  53.1 0.8 collective-permute-done.4.refs_5_
  53.9 0.7 copy-done.3
  54.6 1.0 copy-done.2
  55.6 1.0 copy-done.4
  56.5 3.0 %score.1 = f32[16,16,128]{2,1,0:T(8,128)S(1)} custom-call(bf16[72,2048]{1,0:T(8,128)(2,1)S(1)} %norm.1.refs_0_, bf16[72,2048]{1,0:T(8,128)(2,1)S(1)} %collective-permute-done.refs_1_, bf16[72,2048]{1,0:T(8,128)(2,1)S(1)} %collective-permute-done.1.refs_2_, bf16[72,2048]{1,0:T(8,128)(2,1)S(1)} %collective-permute-done.2.refs_3_, ...), custom_call_target="tpu_custom_call" | custom-call | tf_op jit(solution)/shard_map/score/pallas_call | solution.py:170
  59.5 24.9 %all_to_all.15.in_ref = f32[16,16,128]{2,1,0:T(8,128)S(1)} all-to-all(f32[16,16,128]{2,1,0:T(8,128)S(1)} %score.1), channel_id=1, replica_groups=mesh['cells'=32,'vocab'=16] {'vocab'}, dimensions={0} | all-to-all | bytes 262144 | tf_op jit(solution)/shard_map/all_to_all | solution.py:324
  84.5 0.2 merge.1
  84.7 16.0 %all_to_all.16.in_ref = f32[32,16,128]{2,1,0:T(8,128)S(1)} all-to-all(f32[32,16,128]{2,1,0:T(8,128)S(1)} %merge.1), channel_id=1, replica_groups=mesh['cells'=32,'vocab'=16] {'cells'}, dimensions={0} | all-to-all | bytes 524288 | tf_op jit(solution)/shard_map/all_to_all | solution.py:327
  100.7 0.9 finish.1
  (19 shorter events, 0.0 us)
Async XLA Ops:
  0.6 1.0 copy-start
  3.0 11.3 %copy-start.5 = (bf16[1,4,16,2048]{3,2,1,0:T(8,128)(2,1)S(1)}, bf16[1,4,16,2048]{3,2,1,0:T(8,128)(2,1)}, u32[]{:S(2)}) copy-start(bf16[1,4,16,2048]{3,2,1,0:T(8,128)(2,1)} %param.8) | copy-start | bytes 786436
  3.0 11.3 %copy-start.6 = (f32[1,2048]{1,0:T(1,128)S(1)}, f32[1,2048]{1,0:T(1,128)}, u32[]{:S(2)}) copy-start(f32[1,2048]{1,0:T(1,128)} %clean_ref.1) | copy-start | bytes 24580
  3.0 11.3 %copy-start.7 = (f32[2048]{0:T(1024)S(1)}, f32[2048]{0:T(1024)}, u32[]{:S(2)}) copy-start(f32[2048]{0:T(1024)} %param.12) | copy-start | bytes 24580
  3.0 51.6 %all-to-all-start = ((bf16[32,200,128]{2,1,0:T(8,128)(2,1)}), bf16[32,200,128]{2,1,0:T(8,128)(2,1)S(1)}, u32[]{:S(2)}, u32[]{:S(2)}) async-start(bf16[32,200,128]{2,1,0:T(8,128)(2,1)} %pack.1), calls=%async_computation | async-start | bytes 3276800 | tf_op jit(solution)/shard_map/all_to_all | solution.py:319
  14.3 70.1 %copy-start.8 = (s32[127]{0:T(128)S(1)}, s32[127]{0:T(128)}, u32[]{:S(2)}) copy-start(s32[127]{0:T(128)} %param.9) | copy-start | bytes 1528
  14.3 70.1 %copy-start.9 = (s32[127]{0:T(128)S(1)}, s32[127]{0:T(128)}, u32[]{:S(2)}) copy-start(s32[127]{0:T(128)} %param.10) | copy-start | bytes 1528
  14.5 26.4 %collective-permute-start.2 = (bf16[72,2048]{1,0:T(8,128)(2,1)S(1)}, bf16[72,2048]{1,0:T(8,128)(2,1)S(1)}, u32[]{:S(2)}, u32[]{:S(2)}) collective-permute-start(bf16[72,2048]{1,0:T(8,128)(2,1)S(1)} %norm.1.refs_0_), channel_id=1, source_target_pairs={{0,32},{16,48},{32,64},{48,80},{64,96},{80,112},{96,0},{112,16},{1... | collective-permute-start | bytes 884744 | tf_op jit(solution)/shard_map/ppermute | solution.py:296
  17.8 29.7 %collective-permute-start.1 = (bf16[72,2048]{1,0:T(8,128)(2,1)S(1)}, bf16[72,2048]{1,0:T(8,128)(2,1)S(1)}, u32[]{:S(2)}, u32[]{:S(2)}) collective-permute-start(bf16[72,2048]{1,0:T(8,128)(2,1)S(1)} %norm.1.refs_0_), channel_id=1, source_target_pairs={{0,64},{16,80},{32,96},{48,112},{64,0},{80,16},{96,32},{112,48},{1... | collective-permute-start | bytes 884744 | tf_op jit(solution)/shard_map/ppermute | solution.py:296
  22.1 28.3 %collective-permute-start = (bf16[72,2048]{1,0:T(8,128)(2,1)S(1)}, bf16[72,2048]{1,0:T(8,128)(2,1)S(1)}, u32[]{:S(2)}, u32[]{:S(2)}) collective-permute-start(bf16[72,2048]{1,0:T(8,128)(2,1)S(1)} %norm.1.refs_0_), channel_id=1, source_target_pairs={{0,96},{16,112},{32,0},{48,16},{64,32},{80,48},{96,64},{112,80},{1... | collective-permute-start | bytes 884744 | tf_op jit(solution)/shard_map/ppermute | solution.py:296
  25.2 27.1 %collective-permute-start.3 = (bf16[72,2048]{1,0:T(8,128)(2,1)S(1)}, bf16[72,2048]{1,0:T(8,128)(2,1)S(1)}, u32[]{:S(2)}, u32[]{:S(2)}) collective-permute-start(bf16[72,2048]{1,0:T(8,128)(2,1)S(1)} %norm.1.refs_0_), channel_id=1, source_target_pairs={{0,16},{16,0},{32,48},{48,32},{64,80},{80,64},{96,112},{112,96},{1... | collective-permute-start | bytes 884744 | tf_op jit(solution)/shard_map/ppermute | solution.py:296
  40.9 11.4 %collective-permute-start.6 = (bf16[72,2048]{1,0:T(8,128)(2,1)S(1)}, bf16[72,2048]{1,0:T(8,128)(2,1)S(1)}, u32[]{:S(2)}, u32[]{:S(2)}) collective-permute-start(bf16[72,2048]{1,0:T(8,128)(2,1)S(1)} %collective-permute-done.2.refs_3_), channel_id=1, source_target_pairs={{0,16},{16,0},{32,48},{48,32},{64,80},{80,64},{96,112},{112,96},{1... | collective-permute-start | bytes 884744 | tf_op jit(solution)/shard_map/ppermute | solution.py:296
  47.5 4.8 %collective-permute-start.5 = (bf16[72,2048]{1,0:T(8,128)(2,1)S(1)}, bf16[72,2048]{1,0:T(8,128)(2,1)S(1)}, u32[]{:S(2)}, u32[]{:S(2)}) collective-permute-start(bf16[72,2048]{1,0:T(8,128)(2,1)S(1)} %collective-permute-done.1.refs_2_), channel_id=1, source_target_pairs={{0,16},{16,0},{32,48},{48,32},{64,80},{80,64},{96,112},{112,96},{1... | collective-permute-start | bytes 884744 | tf_op jit(solution)/shard_map/ppermute | solution.py:296
  50.4 3.5 %collective-permute-start.4 = (bf16[72,2048]{1,0:T(8,128)(2,1)S(1)}, bf16[72,2048]{1,0:T(8,128)(2,1)S(1)}, u32[]{:S(2)}, u32[]{:S(2)}) collective-permute-start(bf16[72,2048]{1,0:T(8,128)(2,1)S(1)} %collective-permute-done.refs_1_), channel_id=1, source_target_pairs={{0,16},{16,0},{32,48},{48,32},{64,80},{80,64},{96,112},{112,96},{1... | collective-permute-start | bytes 884744 | tf_op jit(solution)/shard_map/ppermute | solution.py:296
  52.4 0.7 copy-start.1
  53.9 0.7 copy-start.3
  54.6 1.0 copy-start.2
  55.6 1.0 copy-start.4
where the time goes:
time: 102 us
  blocking collectives  40.9 us (40%)
  starting transfers between devices  32.3 us (32%)
  waiting for transfers between devices  16.9 us (17%)
  Pallas kernels  5.65 us (6%)
  local copies, waits for them, and re-layouts  4.36 us (4%)
  between operations  1.45 us (1%)
    all_to_all x1, blocking collectives, on_device(): stats = lax.all_to_all(stats, 'vocab', 0, 0, tiled=True)  24.9 us
    ppermute x7, starting transfers between devices, moved(): return lax.ppermute(value, 'cells', [(i, to(i)) for i in range(PLANE)])  21.7 us
    ppermute x7, waiting for transfers between devices, moved(): return lax.ppermute(value, 'cells', [(i, to(i)) for i in range(PLANE)])  16.9 us
    all_to_all x1, blocking collectives, on_device(): pieces = lax.all_to_all(pieces, 'cells', 0, 0, tiled=True)  16 us
    all_to_all x1, starting transfers between devices, on_device(): weights = lax.all_to_all(packed(unembed), 'cells', 0, 0, tiled=True)  10.6 us
    unnamed x20, local copies, waits for them, and re-layouts  4.36 us
    pallas_call x1, Pallas kernels, scored(): pl.pallas_call(score_kernel, out_shape=jax.ShapeDtypeStruct((copies, 16,...  3 us
  transfers between devices with their start and end apart: 8, of which 3 were waited for; matrix products, arithmetic and copies ran while one was open for 0% of the time, Pallas kernels for 0%

commit v1 on v0

--- a/solution.py
+++ b/solution.py
@@ -105,8 +105,24 @@
     )(answer_ids, clean_resid, delta_table, norm_gain)
 
 
-def score_kernel(*refs):
-    acts, (w_ref, out_ref, a_buf, w_buf, l_buf) = refs[:SUBS], refs[SUBS:]
+def stack_kernel(*refs):
+    acts, out_ref = refs[:SUBS], refs[SUBS]
+    for j in range(SUBS):
+        out_ref[j * ROWS : (j + 1) * ROWS, :] = acts[j][...]
+
+
+def stacked(acts):
+    return pl.pallas_call(
+        stack_kernel,
+        out_shape=jax.ShapeDtypeStruct((SUBS * ROWS, acts[0].shape[1]), BF16),
+        in_specs=[VMEM] * SUBS,
+        out_specs=VMEM,
+        compiler_params=pltpu.CompilerParams(vmem_limit_bytes=8 * MIB),
+        name="stack",
+    )(*acts)
+
+
+def score_kernel(a_ref, w_ref, out_ref, w_buf, l_buf):
     depth = (w_ref.shape[1] - 8) // FULL
     groups = depth // 8
     copies = out_ref.shape[0]
@@ -120,9 +136,7 @@
         left = w_ref[i, FULL * depth :, :].astype(F32)
         pieces = [left] + [pltpu.roll(left, LANES - LEFT * a, 1) for a in range(1, groups)]
         w_buf[rows, FULL * LANES :] = jnp.concatenate(pieces, axis=0).astype(BF16)
-    for j in range(SUBS):
-        a_buf[j * ROWS : (j + 1) * ROWS, :] = acts[j][...]
-    l_buf[...] = jnp.dot(a_buf[...], w_buf[...], preferred_element_type=F32)
+    l_buf[...] = jnp.dot(a_ref[...], w_buf[...], preferred_element_type=F32)
 
     width = (FULL + 1) * LANES
     lane = lanes_of((1, width))
@@ -142,7 +156,7 @@
             sum_clean = jnp.sum(weight, axis=-1, keepdims=True)
             weight = weight * (1.0 / sum_clean)
             clean_lse = max_clean + jnp.log(sum_clean)
-            tail = acts[d * YS + t][KEYS:, 0:LANES].astype(F32)
+            tail = a_ref[at + KEYS : at + ROWS, 0:LANES].astype(F32)
             digits = tail[1:2]
             answer = digits[:, 0:1] * 256.0 + digits[:, 1:2]
             logits = jnp.where(kept, l_buf[at : at + KEYS, :], NEG)
@@ -165,21 +179,20 @@
                 out_ref[i, 4 * k + t : 4 * k + t + 1, :] = line
 
 
-def scored(acts, weights, copies):
+def scored(rows, weights, copies):
     depth = (weights.shape[1] - 8) // FULL
     return pl.pallas_call(
         score_kernel,
         out_shape=jax.ShapeDtypeStruct((copies, 16, LANES), F32),
-        in_specs=[VMEM] * (SUBS + 1),
+        in_specs=[VMEM, VMEM],
         out_specs=VMEM,
         scratch_shapes=[
-            pltpu.VMEM((SUBS * ROWS, acts[0].shape[1]), BF16),
             pltpu.VMEM((PLANE * depth, (FULL + 1) * LANES), BF16),
             pltpu.VMEM((2 * YS * ROWS, (FULL + 1) * LANES), F32),
         ],
-        compiler_params=pltpu.CompilerParams(vmem_limit_bytes=24 * MIB),
+        compiler_params=pltpu.CompilerParams(vmem_limit_bytes=12 * MIB),
         name="score",
-    )(*acts, weights)
+    )(rows, weights)
 
 
 def merged(lse, cross, answer, clean_lse):
@@ -320,7 +333,7 @@
     other = []
     for step in range(YS):
         other.append(moved(same[step], lambda i: i ^ 1))
-    stats = scored(same + other, weights, lax.axis_size("vocab"))
+    stats = scored(stacked(same + other), weights, lax.axis_size("vocab"))
     stats = lax.all_to_all(stats, "vocab", 0, 0, tiled=True)
     layer, pos = layer_index.reshape(1, -1), pos_index.reshape(1, -1)
     pieces = merged_over_vocab(stats, layer, pos, position_count)

time: 102 us -> 101 us (level)
  local copies, waits for them, and re-layouts: 4.36 us -> 1.02 us
  Pallas kernels: 5.65 us -> 7.18 us
    unnamed x20 -> x12, local copies, waits for them, and re-layouts: 4.36 us -> 1.02 us
    pallas_call x1, Pallas kernels: 3 us -> 4.4 us  [scored(): pl.pallas_call(score_kernel, out_shape=jax.ShapeDtypeStruct((copies, 16,...]
where the time goes in v1:
time: 101 us
  blocking collectives  40.3 us (40%)
  starting transfers between devices  32.9 us (33%)
  waiting for transfers between devices  17.6 us (17%)
  Pallas kernels  7.18 us (7%)
  between operations  1.45 us (1%)
  local copies, waits for them, and re-layouts  1.02 us (1%)
    all_to_all x1, blocking collectives, on_device(): stats = lax.all_to_all(stats, 'vocab', 0, 0, tiled=True)  24.3 us
    ppermute x7, starting transfers between devices, moved(): return lax.ppermute(value, 'cells', [(i, to(i)) for i in range(PLANE)])  21.7 us
    ppermute x7, waiting for transfers between devices, moved(): return lax.ppermute(value, 'cells', [(i, to(i)) for i in range(PLANE)])  17.6 us
    all_to_all x1, blocking collectives, on_device(): pieces = lax.all_to_all(pieces, 'cells', 0, 0, tiled=True)  16 us
    all_to_all x1, starting transfers between devices, on_device(): weights = lax.all_to_all(packed(unembed), 'cells', 0, 0, tiled=True)  11.3 us
    pallas_call x1, Pallas kernels, scored(): pl.pallas_call(score_kernel, out_shape=jax.ShapeDtypeStruct((copies, 16,...  4.4 us
  transfers between devices with their start and end apart: 8, of which 3 were waited for; matrix products, arithmetic and copies ran while one was open for 0% of the time, Pallas kernels for 0%

profile of v1, /device:TPU:1, one launch (start us, length us, event | category | flops | bytes accessed | tf_op | source)
XLA Modules:
  0.0 100.5 jit_solution(6069564489032247836)
XLA Ops:
  0.6 1.0 copy-done
  1.6 1.4 %pack.1 = bf16[32,200,128]{2,1,0:T(8,128)(2,1)} custom-call(bf16[64,3200]{1,0:T(8,128)(2,1)S(1)} %copy-done), custom_call_target="tpu_custom_call" | custom-call | tf_op jit(solution)/shard_map/pack/pallas_call | solution.py:52
  3.0 11.3 %all-to-all-start = ((bf16[32,200,128]{2,1,0:T(8,128)(2,1)}), bf16[32,200,128]{2,1,0:T(8,128)(2,1)}, u32[]{:S(2)}, u32[]{:S(2)}) async-start(bf16[32,200,128]{2,1,0:T(8,128)(2,1)} %pack.1), calls=%async_computation | async-start | bytes 3276800 | tf_op jit(solution)/shard_map/all_to_all | solution.py:332
  15.0 0.2 norm.1.refs_0_
  15.1 3.3 %collective-permute-start.2 = (bf16[72,2048]{1,0:T(8,128)(2,1)S(1)}, bf16[72,2048]{1,0:T(8,128)(2,1)S(1)}, u32[]{:S(2)}, u32[]{:S(2)}) collective-permute-start(bf16[72,2048]{1,0:T(8,128)(2,1)S(1)} %norm.1.refs_0_), channel_id=1, source_target_pairs={{0,32},{16,48},{32,64},{48,80},{64,96},{80,112},{96,0},{112,16},{1... | collective-permute-start | bytes 884744 | tf_op jit(solution)/shard_map/ppermute | solution.py:309
  18.4 4.3 %collective-permute-start.1 = (bf16[72,2048]{1,0:T(8,128)(2,1)S(1)}, bf16[72,2048]{1,0:T(8,128)(2,1)S(1)}, u32[]{:S(2)}, u32[]{:S(2)}) collective-permute-start(bf16[72,2048]{1,0:T(8,128)(2,1)S(1)} %norm.1.refs_0_), channel_id=1, source_target_pairs={{0,64},{16,80},{32,96},{48,112},{64,0},{80,16},{96,32},{112,48},{1... | collective-permute-start | bytes 884744 | tf_op jit(solution)/shard_map/ppermute | solution.py:309
  22.8 3.1 %collective-permute-start = (bf16[72,2048]{1,0:T(8,128)(2,1)S(1)}, bf16[72,2048]{1,0:T(8,128)(2,1)S(1)}, u32[]{:S(2)}, u32[]{:S(2)}) collective-permute-start(bf16[72,2048]{1,0:T(8,128)(2,1)S(1)} %norm.1.refs_0_), channel_id=1, source_target_pairs={{0,96},{16,112},{32,0},{48,16},{64,32},{80,48},{96,64},{112,80},{1... | collective-permute-start | bytes 884744 | tf_op jit(solution)/shard_map/ppermute | solution.py:309
  25.8 3.1 %collective-permute-start.3 = (bf16[72,2048]{1,0:T(8,128)(2,1)S(1)}, bf16[72,2048]{1,0:T(8,128)(2,1)S(1)}, u32[]{:S(2)}, u32[]{:S(2)}) collective-permute-start(bf16[72,2048]{1,0:T(8,128)(2,1)S(1)} %norm.1.refs_0_), channel_id=1, source_target_pairs={{0,16},{16,0},{32,48},{48,32},{64,80},{80,64},{96,112},{112,96},{1... | collective-permute-start | bytes 884744 | tf_op jit(solution)/shard_map/ppermute | solution.py:309
  29.0 12.5 %collective-permute-done.2.refs_3_ = bf16[72,2048]{1,0:T(8,128)(2,1)S(1)} collective-permute-done((bf16[72,2048]{1,0:T(8,128)(2,1)S(1)}, bf16[72,2048]{1,0:T(8,128)(2,1)S(1)}, u32[]{:S(2)}, u32[]{:S(2)}) %collective-permute-start.2) | collective-permute-done | bytes 294944 | tf_op jit(solution)/shard_map/ppermute | solution.py:309
  41.5 3.1 %collective-permute-start.6 = (bf16[72,2048]{1,0:T(8,128)(2,1)S(1)}, bf16[72,2048]{1,0:T(8,128)(2,1)S(1)}, u32[]{:S(2)}, u32[]{:S(2)}) collective-permute-start(bf16[72,2048]{1,0:T(8,128)(2,1)S(1)} %collective-permute-done.2.refs_3_), channel_id=1, source_target_pairs={{0,16},{16,0},{32,48},{48,32},{64,80},{80,64},{96,112},{112,96},{1... | collective-permute-start | bytes 884744 | tf_op jit(solution)/shard_map/ppermute | solution.py:309
  44.6 3.5 %collective-permute-done.1.refs_2_ = bf16[72,2048]{1,0:T(8,128)(2,1)S(1)} collective-permute-done((bf16[72,2048]{1,0:T(8,128)(2,1)S(1)}, bf16[72,2048]{1,0:T(8,128)(2,1)S(1)}, u32[]{:S(2)}, u32[]{:S(2)}) %collective-permute-start.1) | collective-permute-done | bytes 294944 | tf_op jit(solution)/shard_map/ppermute | solution.py:309
  48.1 2.9 %collective-permute-start.5 = (bf16[72,2048]{1,0:T(8,128)(2,1)S(1)}, bf16[72,2048]{1,0:T(8,128)(2,1)S(1)}, u32[]{:S(2)}, u32[]{:S(2)}) collective-permute-start(bf16[72,2048]{1,0:T(8,128)(2,1)S(1)} %collective-permute-done.1.refs_2_), channel_id=1, source_target_pairs={{0,16},{16,0},{32,48},{48,32},{64,80},{80,64},{96,112},{112,96},{1... | collective-permute-start | bytes 884744 | tf_op jit(solution)/shard_map/ppermute | solution.py:309
  51.0 0.0 collective-permute-done.refs_1_
  51.0 1.9 %collective-permute-start.4 = (bf16[72,2048]{1,0:T(8,128)(2,1)S(1)}, bf16[72,2048]{1,0:T(8,128)(2,1)S(1)}, u32[]{:S(2)}, u32[]{:S(2)}) collective-permute-start(bf16[72,2048]{1,0:T(8,128)(2,1)S(1)} %collective-permute-done.refs_1_), channel_id=1, source_target_pairs={{0,16},{16,0},{32,48},{48,32},{64,80},{80,64},{96,112},{112,96},{1... | collective-permute-start | bytes 884744 | tf_op jit(solution)/shard_map/ppermute | solution.py:309
  52.9 0.0 collective-permute-done.3.refs_4_
  53.0 1.5 %collective-permute-done.4.refs_5_ = bf16[72,2048]{1,0:T(8,128)(2,1)S(1)} collective-permute-done((bf16[72,2048]{1,0:T(8,128)(2,1)S(1)}, bf16[72,2048]{1,0:T(8,128)(2,1)S(1)}, u32[]{:S(2)}, u32[]{:S(2)}) %collective-permute-start.4) | collective-permute-done | bytes 294944 | tf_op jit(solution)/shard_map/ppermute | solution.py:309
  54.5 0.2 stack.1.a_ref
  54.7 0.0 copy-start.4
  54.7 0.0 copy-start.5
  54.7 4.4 %score.1 = f32[16,16,128]{2,1,0:T(8,128)S(1)} custom-call(bf16[576,2048]{1,0:T(8,128)(2,1)S(1)} %stack.1.a_ref, bf16[32,200,128]{2,1,0:T(8,128)(2,1)} %all-to-all-done.w_ref), custom_call_target="tpu_custom_call" | custom-call | tf_op jit(solution)/shard_map/score/pallas_call | solution.py:184
  59.1 24.3 %all_to_all.15.in_ref = f32[16,16,128]{2,1,0:T(8,128)S(1)} all-to-all(f32[16,16,128]{2,1,0:T(8,128)S(1)} %score.1), channel_id=1, replica_groups=mesh['cells'=32,'vocab'=16] {'vocab'}, dimensions={0} | all-to-all | bytes 262144 | tf_op jit(solution)/shard_map/all_to_all | solution.py:337
  83.4 0.2 merge.1
  83.6 16.0 %all_to_all.16.in_ref = f32[32,16,128]{2,1,0:T(8,128)S(1)} all-to-all(f32[32,16,128]{2,1,0:T(8,128)S(1)} %merge.1), channel_id=1, replica_groups=mesh['cells'=32,'vocab'=16] {'cells'}, dimensions={0} | all-to-all | bytes 524288 | tf_op jit(solution)/shard_map/all_to_all | solution.py:340
  99.6 0.9 finish.1
  (12 shorter events, 0.0 us)
Async XLA Ops:
  0.6 1.0 copy-start
  3.0 11.9 %copy-start.1 = (bf16[1,4,16,2048]{3,2,1,0:T(8,128)(2,1)S(1)}, bf16[1,4,16,2048]{3,2,1,0:T(8,128)(2,1)}, u32[]{:S(2)}) copy-start(bf16[1,4,16,2048]{3,2,1,0:T(8,128)(2,1)} %param.8) | copy-start | bytes 786436
  3.0 11.9 %copy-start.2 = (f32[1,2048]{1,0:T(1,128)S(1)}, f32[1,2048]{1,0:T(1,128)}, u32[]{:S(2)}) copy-start(f32[1,2048]{1,0:T(1,128)} %clean_ref.1) | copy-start | bytes 24580
  3.0 11.9 %copy-start.3 = (f32[2048]{0:T(1024)S(1)}, f32[2048]{0:T(1024)}, u32[]{:S(2)}) copy-start(f32[2048]{0:T(1024)} %param.12) | copy-start | bytes 24580
  3.0 51.7 %all-to-all-start = ((bf16[32,200,128]{2,1,0:T(8,128)(2,1)}), bf16[32,200,128]{2,1,0:T(8,128)(2,1)}, u32[]{:S(2)}, u32[]{:S(2)}) async-start(bf16[32,200,128]{2,1,0:T(8,128)(2,1)} %pack.1), calls=%async_computation | async-start | bytes 3276800 | tf_op jit(solution)/shard_map/all_to_all | solution.py:332
  15.1 26.4 %collective-permute-start.2 = (bf16[72,2048]{1,0:T(8,128)(2,1)S(1)}, bf16[72,2048]{1,0:T(8,128)(2,1)S(1)}, u32[]{:S(2)}, u32[]{:S(2)}) collective-permute-start(bf16[72,2048]{1,0:T(8,128)(2,1)S(1)} %norm.1.refs_0_), channel_id=1, source_target_pairs={{0,32},{16,48},{32,64},{48,80},{64,96},{80,112},{96,0},{112,16},{1... | collective-permute-start | bytes 884744 | tf_op jit(solution)/shard_map/ppermute | solution.py:309
  18.4 29.7 %collective-permute-start.1 = (bf16[72,2048]{1,0:T(8,128)(2,1)S(1)}, bf16[72,2048]{1,0:T(8,128)(2,1)S(1)}, u32[]{:S(2)}, u32[]{:S(2)}) collective-permute-start(bf16[72,2048]{1,0:T(8,128)(2,1)S(1)} %norm.1.refs_0_), channel_id=1, source_target_pairs={{0,64},{16,80},{32,96},{48,112},{64,0},{80,16},{96,32},{112,48},{1... | collective-permute-start | bytes 884744 | tf_op jit(solution)/shard_map/ppermute | solution.py:309
  22.8 28.2 %collective-permute-start = (bf16[72,2048]{1,0:T(8,128)(2,1)S(1)}, bf16[72,2048]{1,0:T(8,128)(2,1)S(1)}, u32[]{:S(2)}, u32[]{:S(2)}) collective-permute-start(bf16[72,2048]{1,0:T(8,128)(2,1)S(1)} %norm.1.refs_0_), channel_id=1, source_target_pairs={{0,96},{16,112},{32,0},{48,16},{64,32},{80,48},{96,64},{112,80},{1... | collective-permute-start | bytes 884744 | tf_op jit(solution)/shard_map/ppermute | solution.py:309
  25.8 27.1 %collective-permute-start.3 = (bf16[72,2048]{1,0:T(8,128)(2,1)S(1)}, bf16[72,2048]{1,0:T(8,128)(2,1)S(1)}, u32[]{:S(2)}, u32[]{:S(2)}) collective-permute-start(bf16[72,2048]{1,0:T(8,128)(2,1)S(1)} %norm.1.refs_0_), channel_id=1, source_target_pairs={{0,16},{16,0},{32,48},{48,32},{64,80},{80,64},{96,112},{112,96},{1... | collective-permute-start | bytes 884744 | tf_op jit(solution)/shard_map/ppermute | solution.py:309
  41.5 11.4 %collective-permute-start.6 = (bf16[72,2048]{1,0:T(8,128)(2,1)S(1)}, bf16[72,2048]{1,0:T(8,128)(2,1)S(1)}, u32[]{:S(2)}, u32[]{:S(2)}) collective-permute-start(bf16[72,2048]{1,0:T(8,128)(2,1)S(1)} %collective-permute-done.2.refs_3_), channel_id=1, source_target_pairs={{0,16},{16,0},{32,48},{48,32},{64,80},{80,64},{96,112},{112,96},{1... | collective-permute-start | bytes 884744 | tf_op jit(solution)/shard_map/ppermute | solution.py:309
  48.1 4.8 %collective-permute-start.5 = (bf16[72,2048]{1,0:T(8,128)(2,1)S(1)}, bf16[72,2048]{1,0:T(8,128)(2,1)S(1)}, u32[]{:S(2)}, u32[]{:S(2)}) collective-permute-start(bf16[72,2048]{1,0:T(8,128)(2,1)S(1)} %collective-permute-done.1.refs_2_), channel_id=1, source_target_pairs={{0,16},{16,0},{32,48},{48,32},{64,80},{80,64},{96,112},{112,96},{1... | collective-permute-start | bytes 884744 | tf_op jit(solution)/shard_map/ppermute | solution.py:309
  51.0 3.5 %collective-permute-start.4 = (bf16[72,2048]{1,0:T(8,128)(2,1)S(1)}, bf16[72,2048]{1,0:T(8,128)(2,1)S(1)}, u32[]{:S(2)}, u32[]{:S(2)}) collective-permute-start(bf16[72,2048]{1,0:T(8,128)(2,1)S(1)} %collective-permute-done.refs_1_), channel_id=1, source_target_pairs={{0,16},{16,0},{32,48},{48,32},{64,80},{80,64},{96,112},{112,96},{1... | collective-permute-start | bytes 884744 | tf_op jit(solution)/shard_map/ppermute | solution.py:309
  54.7 28.7 %copy-start.4 = (s32[127]{0:T(128)S(1)}, s32[127]{0:T(128)}, u32[]{:S(2)}) copy-start(s32[127]{0:T(128)} %param.9) | copy-start | bytes 1528
  54.7 28.7 %copy-start.5 = (s32[127]{0:T(128)S(1)}, s32[127]{0:T(128)}, u32[]{:S(2)}) copy-start(s32[127]{0:T(128)} %param.10) | copy-start | bytes 1528

commit v2 on v1

--- a/solution.py
+++ b/solution.py
@@ -28,7 +28,19 @@
     return lax.broadcasted_iota(jnp.int32, shape, len(shape) - 1)
 
 
-def pack_kernel(u_ref, out_ref):
+def key_hits(layer_ref, pos_ref, position_count):
+    flat = layer_ref[...] * position_count + pos_ref[...]
+    key = lax.broadcasted_iota(jnp.int32, (LANES, flat.shape[1]), 0)
+    return (key == flat).astype(F32)
+
+
+def as_line(column):
+    square = (LANES, LANES)
+    eye = lax.broadcasted_iota(jnp.int32, square, 0) == lanes_of(square)
+    return jnp.sum(jnp.where(eye, column, 0.0), axis=0, keepdims=True)
+
+
+def pack_columns(u_ref, out_ref):
     depth = u_ref.shape[0]
     groups = depth // 8
     last = u_ref[:, SUBS * FULL * LANES :].astype(F32)
@@ -47,31 +59,7 @@
             out_ref[to, FULL * depth :, :] = left
 
 
-def packed(unembed):
-    depth = unembed.shape[0]
-    return pl.pallas_call(
-        pack_kernel,
-        out_shape=jax.ShapeDtypeStruct((PLANE, FULL * depth + 8, LANES), BF16),
-        in_specs=[VMEM],
-        out_specs=VMEM,
-        compiler_params=pltpu.CompilerParams(vmem_limit_bytes=8 * MIB),
-        name="pack",
-    )(unembed)
-
-
-def key_hits(layer_ref, pos_ref, position_count):
-    flat = layer_ref[...] * position_count + pos_ref[...]
-    key = lax.broadcasted_iota(jnp.int32, (LANES, flat.shape[1]), 0)
-    return (key == flat).astype(F32)
-
-
-def as_line(column):
-    square = (LANES, LANES)
-    eye = lax.broadcasted_iota(jnp.int32, square, 0) == lanes_of(square)
-    return jnp.sum(jnp.where(eye, column, 0.0), axis=0, keepdims=True)
-
-
-def norm_kernel(answer_ref, clean_ref, delta_ref, gain_ref, act_ref):
+def norm_rows(answer_ref, clean_ref, delta_ref, gain_ref, act_ref):
     features = clean_ref.shape[1]
     clean = clean_ref[...]
     gain = gain_ref[...]
@@ -80,7 +68,7 @@
         mean_square = jnp.sum(values * values, axis=-1, keepdims=True) * (1.0 / features)
         return values * lax.rsqrt(mean_square + 1e-06) * gain
 
-    patched = normed(clean + delta_ref[...].astype(F32)).astype(BF16)
+    act_ref[:KEYS, :] = normed(clean + delta_ref[...].astype(F32)).astype(BF16)
     answer = answer_ref[0]
     high = lax.shift_right_logical(answer, 8).astype(F32)
     low = (answer & 255).astype(F32)
@@ -88,21 +76,42 @@
     row = lax.broadcasted_iota(jnp.int32, shape, 0)
     lane = lanes_of(shape)
     digits = jnp.where(lane == 0, high, jnp.where(lane == 1, low, 0.0))
-    tail = jnp.where(row == 0, normed(clean), jnp.where(row == 1, digits, 0.0)).astype(BF16)
-    act_ref[:KEYS, :] = patched
-    act_ref[KEYS:, :] = tail
-
-
-def normed_rows(answer_ids, clean_resid, delta_table, norm_gain):
-    features = clean_resid.shape[1]
-    return pl.pallas_call(
-        norm_kernel,
-        out_shape=jax.ShapeDtypeStruct((ROWS, features), BF16),
-        in_specs=[SMEM, VMEM, VMEM, VMEM],
-        out_specs=VMEM,
-        compiler_params=pltpu.CompilerParams(vmem_limit_bytes=8 * MIB),
-        name="norm",
-    )(answer_ids, clean_resid, delta_table, norm_gain)
+    tail = jnp.where(row == 0, normed(clean), jnp.where(row == 1, digits, 0.0))
+    act_ref[KEYS:, :] = tail.astype(BF16)
+
+
+def prepare_kernel(answer_ref, *refs):
+    sources, (act_ref, pack_ref), buffers, sems = refs[:4], refs[4:6], refs[6:10], refs[10]
+    copies = [
+        pltpu.make_async_copy(source, buffer, sems.at[k])
+        for k, (source, buffer) in enumerate(zip(sources, buffers))
+    ]
+    for copy in copies:
+        copy.start()
+    for copy in copies[:3]:
+        copy.wait()
+    clean, delta, gain, columns = buffers
+    norm_rows(answer_ref, clean, delta, gain, act_ref)
+    copies[3].wait()
+    pack_columns(columns, pack_ref)
+
+
+def prepared(answer_ids, clean_resid, delta_table, norm_gain, unembed):
+    arrays = (clean_resid, delta_table, norm_gain, unembed)
+    depth = unembed.shape[0]
+    return pl.pallas_call(
+        prepare_kernel,
+        out_shape=(
+            jax.ShapeDtypeStruct((ROWS, clean_resid.shape[1]), BF16),
+            jax.ShapeDtypeStruct((PLANE, FULL * depth + 8, LANES), BF16),
+        ),
+        in_specs=[SMEM] + [pl.BlockSpec(memory_space=pltpu.HBM)] * 4,
+        out_specs=(VMEM, VMEM),
+        scratch_shapes=[pltpu.VMEM(array.shape, array.dtype) for array in arrays]
+        + [pltpu.SemaphoreType.DMA((4,))],
+        compiler_params=pltpu.CompilerParams(vmem_limit_bytes=67043328),
+        name="prepare",
+    )(answer_ids, *arrays)
 
 
 def stack_kernel(*refs):
@@ -320,16 +329,17 @@
 def on_device(clean_resid, path_delta, layer_index, pos_index, answer_ids, norm_gain, unembed):
     position_count = path_delta.shape[2]
     features = clean_resid.shape[1]
-    act = normed_rows(
+    act, sent = prepared(
         answer_ids,
         clean_resid,
         path_delta.reshape(KEYS, features),
         norm_gain.reshape(1, features),
+        unembed,
     )
     same = [act]
     for step in range(1, YS):
         same.append(moved(act, along_y(step)))
-    weights = lax.all_to_all(packed(unembed), "cells", 0, 0, tiled=True)
+    weights = lax.all_to_all(sent, "cells", 0, 0, tiled=True)
     other = []
     for step in range(YS):
         other.append(moved(same[step], lambda i: i ^ 1))

time: 101 us -> 102 us (level)
    pallas_call x2 -> x1, Pallas kernels: 1.56 us -> 2.56 us  [prepared(): pl.pallas_call(prepare_kernel, out_shape=(jax.ShapeDtypeStruct((ROWS, cle...]
where the time goes in v2:
time: 102 us; the launch traced here: 101 us
  blocking collectives  40.3 us (40%)
  starting transfers between devices  33 us (32%)
  waiting for transfers between devices  18.4 us (18%)
  Pallas kernels  8.19 us (8%)
  between operations  1.44 us (1%)
    all_to_all x1, blocking collectives, on_device(): stats = lax.all_to_all(stats, 'vocab', 0, 0, tiled=True)  24.3 us
    ppermute x7, starting transfers between devices, moved(): return lax.ppermute(value, 'cells', [(i, to(i)) for i in range(PLANE)])  21.7 us
    ppermute x7, waiting for transfers between devices, moved(): return lax.ppermute(value, 'cells', [(i, to(i)) for i in range(PLANE)])  18.4 us
    all_to_all x1, blocking collectives, on_device(): pieces = lax.all_to_all(pieces, 'cells', 0, 0, tiled=True)  16 us
    all_to_all x1, starting transfers between devices, on_device(): weights = lax.all_to_all(sent, 'cells', 0, 0, tiled=True)  11.3 us
    pallas_call x1, Pallas kernels, scored(): pl.pallas_call(score_kernel, out_shape=jax.ShapeDtypeStruct((copies, 16,...  4.4 us
    pallas_call x1, Pallas kernels, prepared(): pl.pallas_call(prepare_kernel, out_shape=(jax.ShapeDtypeStruct((ROWS, cle...  2.56 us
  transfers between devices with their start and end apart: 8, of which 3 were waited for; matrix products, arithmetic and copies ran while one was open for 0% of the time, Pallas kernels for 0%

profile of v2, /device:TPU:1, one launch (start us, length us, event | category | flops | bytes accessed | tf_op | source)
XLA Modules:
  0.0 101.4 jit_solution(18260321552761228778)
XLA Ops:
  1.3 2.6 %prepare.1 = (bf16[72,2048]{1,0:T(8,128)(2,1)}, bf16[32,200,128]{2,1,0:T(8,128)(2,1)}) custom-call(s32[1]{0:T(128)S(6)} %copy.10.answer_ref, f32[1,2048]{1,0:T(1,128)} %refs_0_.1, bf16[64,2048]{1,0:T(8,128)(2,1)} %bitcast.9, f32[1,2048]{1,0:T(1,128)} %bitcast.10, bf16[64,3200]{1,0:T(8,128)(2,1)} %refs_3_.1), custom_call_target="tpu_custom_call" | custom-call | tf_op jit(solution)/shard_map/prepare/pallas_call | solution.py:102
  3.9 11.3 %all-to-all-start = ((bf16[32,200,128]{2,1,0:T(8,128)(2,1)}), bf16[32,200,128]{2,1,0:T(8,128)(2,1)}, u32[]{:S(2)}, u32[]{:S(2)}) async-start(bf16[32,200,128]{2,1,0:T(8,128)(2,1)} %get-tuple-element.9), calls=%async_computation | async-start | bytes 3276800 | tf_op jit(solution)/shard_map/all_to_all | solution.py:342
  15.2 3.3 %collective-permute-start.2 = (bf16[72,2048]{1,0:T(8,128)(2,1)S(1)}, bf16[72,2048]{1,0:T(8,128)(2,1)S(1)}, u32[]{:S(2)}, u32[]{:S(2)}) collective-permute-start(bf16[72,2048]{1,0:T(8,128)(2,1)S(1)} %copy-done), channel_id=1, source_target_pairs={{0,32},{16,48},{32,64},{48,80},{64,96},{80,112},{96,0},{112,16},{1... | collective-permute-start | bytes 884744 | tf_op jit(solution)/shard_map/ppermute | solution.py:318
  18.4 4.3 %collective-permute-start.1 = (bf16[72,2048]{1,0:T(8,128)(2,1)S(1)}, bf16[72,2048]{1,0:T(8,128)(2,1)S(1)}, u32[]{:S(2)}, u32[]{:S(2)}) collective-permute-start(bf16[72,2048]{1,0:T(8,128)(2,1)S(1)} %copy-done), channel_id=1, source_target_pairs={{0,64},{16,80},{32,96},{48,112},{64,0},{80,16},{96,32},{112,48},{1... | collective-permute-start | bytes 884744 | tf_op jit(solution)/shard_map/ppermute | solution.py:318
  22.8 3.1 %collective-permute-start = (bf16[72,2048]{1,0:T(8,128)(2,1)S(1)}, bf16[72,2048]{1,0:T(8,128)(2,1)S(1)}, u32[]{:S(2)}, u32[]{:S(2)}) collective-permute-start(bf16[72,2048]{1,0:T(8,128)(2,1)S(1)} %copy-done), channel_id=1, source_target_pairs={{0,96},{16,112},{32,0},{48,16},{64,32},{80,48},{96,64},{112,80},{1... | collective-permute-start | bytes 884744 | tf_op jit(solution)/shard_map/ppermute | solution.py:318
  25.9 3.1 %collective-permute-start.3 = (bf16[72,2048]{1,0:T(8,128)(2,1)S(1)}, bf16[72,2048]{1,0:T(8,128)(2,1)S(1)}, u32[]{:S(2)}, u32[]{:S(2)}) collective-permute-start(bf16[72,2048]{1,0:T(8,128)(2,1)S(1)} %copy-done), channel_id=1, source_target_pairs={{0,16},{16,0},{32,48},{48,32},{64,80},{80,64},{96,112},{112,96},{1... | collective-permute-start | bytes 884744 | tf_op jit(solution)/shard_map/ppermute | solution.py:318
  29.0 13.4 %collective-permute-done.2.refs_3_ = bf16[72,2048]{1,0:T(8,128)(2,1)S(1)} collective-permute-done((bf16[72,2048]{1,0:T(8,128)(2,1)S(1)}, bf16[72,2048]{1,0:T(8,128)(2,1)S(1)}, u32[]{:S(2)}, u32[]{:S(2)}) %collective-permute-start.2) | collective-permute-done | bytes 294944 | tf_op jit(solution)/shard_map/ppermute | solution.py:318
  42.4 3.1 %collective-permute-start.6 = (bf16[72,2048]{1,0:T(8,128)(2,1)S(1)}, bf16[72,2048]{1,0:T(8,128)(2,1)S(1)}, u32[]{:S(2)}, u32[]{:S(2)}) collective-permute-start(bf16[72,2048]{1,0:T(8,128)(2,1)S(1)} %collective-permute-done.2.refs_3_), channel_id=1, source_target_pairs={{0,16},{16,0},{32,48},{48,32},{64,80},{80,64},{96,112},{112,96},{1... | collective-permute-start | bytes 884744 | tf_op jit(solution)/shard_map/ppermute | solution.py:318
  45.5 3.5 %collective-permute-done.1.refs_2_ = bf16[72,2048]{1,0:T(8,128)(2,1)S(1)} collective-permute-done((bf16[72,2048]{1,0:T(8,128)(2,1)S(1)}, bf16[72,2048]{1,0:T(8,128)(2,1)S(1)}, u32[]{:S(2)}, u32[]{:S(2)}) %collective-permute-start.1) | collective-permute-done | bytes 294944 | tf_op jit(solution)/shard_map/ppermute | solution.py:318
  49.0 2.9 %collective-permute-start.5 = (bf16[72,2048]{1,0:T(8,128)(2,1)S(1)}, bf16[72,2048]{1,0:T(8,128)(2,1)S(1)}, u32[]{:S(2)}, u32[]{:S(2)}) collective-permute-start(bf16[72,2048]{1,0:T(8,128)(2,1)S(1)} %collective-permute-done.1.refs_2_), channel_id=1, source_target_pairs={{0,16},{16,0},{32,48},{48,32},{64,80},{80,64},{96,112},{112,96},{1... | collective-permute-start | bytes 884744 | tf_op jit(solution)/shard_map/ppermute | solution.py:318
  51.9 0.0 collective-permute-done.refs_1_
  51.9 1.9 %collective-permute-start.4 = (bf16[72,2048]{1,0:T(8,128)(2,1)S(1)}, bf16[72,2048]{1,0:T(8,128)(2,1)S(1)}, u32[]{:S(2)}, u32[]{:S(2)}) collective-permute-start(bf16[72,2048]{1,0:T(8,128)(2,1)S(1)} %collective-permute-done.refs_1_), channel_id=1, source_target_pairs={{0,16},{16,0},{32,48},{48,32},{64,80},{80,64},{96,112},{112,96},{1... | collective-permute-start | bytes 884744 | tf_op jit(solution)/shard_map/ppermute | solution.py:318
  53.8 0.0 collective-permute-done.3.refs_4_
  53.8 0.0 collective-permute-done.6.refs_7_
  53.8 0.0 collective-permute-done.5.refs_6_
  53.8 1.5 %collective-permute-done.4.refs_5_ = bf16[72,2048]{1,0:T(8,128)(2,1)S(1)} collective-permute-done((bf16[72,2048]{1,0:T(8,128)(2,1)S(1)}, bf16[72,2048]{1,0:T(8,128)(2,1)S(1)}, u32[]{:S(2)}, u32[]{:S(2)}) %collective-permute-start.4) | collective-permute-done | bytes 294944 | tf_op jit(solution)/shard_map/ppermute | solution.py:318
  55.4 0.2 stack.1.a_ref
  55.5 0.0 copy-start.1
  55.5 0.0 copy-start.2
  55.5 4.4 %score.1 = f32[16,16,128]{2,1,0:T(8,128)S(1)} custom-call(bf16[576,2048]{1,0:T(8,128)(2,1)S(1)} %stack.1.a_ref, bf16[32,200,128]{2,1,0:T(8,128)(2,1)} %all-to-all-done.w_ref), custom_call_target="tpu_custom_call" | custom-call | tf_op jit(solution)/shard_map/score/pallas_call | solution.py:193
  59.9 24.3 %all_to_all.15.in_ref = f32[16,16,128]{2,1,0:T(8,128)S(1)} all-to-all(f32[16,16,128]{2,1,0:T(8,128)S(1)} %score.1), channel_id=1, replica_groups=mesh['cells'=32,'vocab'=16] {'vocab'}, dimensions={0} | all-to-all | bytes 262144 | tf_op jit(solution)/shard_map/all_to_all | solution.py:347
  84.2 0.2 merge.1
  84.4 16.0 %all_to_all.16.in_ref = f32[32,16,128]{2,1,0:T(8,128)S(1)} all-to-all(f32[32,16,128]{2,1,0:T(8,128)S(1)} %merge.1), channel_id=1, replica_groups=mesh['cells'=32,'vocab'=16] {'cells'}, dimensions={0} | all-to-all | bytes 524288 | tf_op jit(solution)/shard_map/all_to_all | solution.py:350
  100.5 0.9 finish.1
  (5 shorter events, 0.0 us)
Async XLA Ops:
  3.8 11.3 %copy-start = (bf16[72,2048]{1,0:T(8,128)(2,1)S(1)}, bf16[72,2048]{1,0:T(8,128)(2,1)}, u32[]{:S(2)}) copy-start(bf16[72,2048]{1,0:T(8,128)(2,1)} %get-tuple-element.8.refs_0_) | copy-start | bytes 884740
  3.9 51.7 %all-to-all-start = ((bf16[32,200,128]{2,1,0:T(8,128)(2,1)}), bf16[32,200,128]{2,1,0:T(8,128)(2,1)}, u32[]{:S(2)}, u32[]{:S(2)}) async-start(bf16[32,200,128]{2,1,0:T(8,128)(2,1)} %get-tuple-element.9), calls=%async_computation | async-start | bytes 3276800 | tf_op jit(solution)/shard_map/all_to_all | solution.py:342
  15.2 27.2 %collective-permute-start.2 = (bf16[72,2048]{1,0:T(8,128)(2,1)S(1)}, bf16[72,2048]{1,0:T(8,128)(2,1)S(1)}, u32[]{:S(2)}, u32[]{:S(2)}) collective-permute-start(bf16[72,2048]{1,0:T(8,128)(2,1)S(1)} %copy-done), channel_id=1, source_target_pairs={{0,32},{16,48},{32,64},{48,80},{64,96},{80,112},{96,0},{112,16},{1... | collective-permute-start | bytes 884744 | tf_op jit(solution)/shard_map/ppermute | solution.py:318
  18.4 30.6 %collective-permute-start.1 = (bf16[72,2048]{1,0:T(8,128)(2,1)S(1)}, bf16[72,2048]{1,0:T(8,128)(2,1)S(1)}, u32[]{:S(2)}, u32[]{:S(2)}) collective-permute-start(bf16[72,2048]{1,0:T(8,128)(2,1)S(1)} %copy-done), channel_id=1, source_target_pairs={{0,64},{16,80},{32,96},{48,112},{64,0},{80,16},{96,32},{112,48},{1... | collective-permute-start | bytes 884744 | tf_op jit(solution)/shard_map/ppermute | solution.py:318
  22.8 29.1 %collective-permute-start = (bf16[72,2048]{1,0:T(8,128)(2,1)S(1)}, bf16[72,2048]{1,0:T(8,128)(2,1)S(1)}, u32[]{:S(2)}, u32[]{:S(2)}) collective-permute-start(bf16[72,2048]{1,0:T(8,128)(2,1)S(1)} %copy-done), channel_id=1, source_target_pairs={{0,96},{16,112},{32,0},{48,16},{64,32},{80,48},{96,64},{112,80},{1... | collective-permute-start | bytes 884744 | tf_op jit(solution)/shard_map/ppermute | solution.py:318
  25.9 27.9 %collective-permute-start.3 = (bf16[72,2048]{1,0:T(8,128)(2,1)S(1)}, bf16[72,2048]{1,0:T(8,128)(2,1)S(1)}, u32[]{:S(2)}, u32[]{:S(2)}) collective-permute-start(bf16[72,2048]{1,0:T(8,128)(2,1)S(1)} %copy-done), channel_id=1, source_target_pairs={{0,16},{16,0},{32,48},{48,32},{64,80},{80,64},{96,112},{112,96},{1... | collective-permute-start | bytes 884744 | tf_op jit(solution)/shard_map/ppermute | solution.py:318
  42.4 11.5 %collective-permute-start.6 = (bf16[72,2048]{1,0:T(8,128)(2,1)S(1)}, bf16[72,2048]{1,0:T(8,128)(2,1)S(1)}, u32[]{:S(2)}, u32[]{:S(2)}) collective-permute-start(bf16[72,2048]{1,0:T(8,128)(2,1)S(1)} %collective-permute-done.2.refs_3_), channel_id=1, source_target_pairs={{0,16},{16,0},{32,48},{48,32},{64,80},{80,64},{96,112},{112,96},{1... | collective-permute-start | bytes 884744 | tf_op jit(solution)/shard_map/ppermute | solution.py:318
  49.0 4.8 %collective-permute-start.5 = (bf16[72,2048]{1,0:T(8,128)(2,1)S(1)}, bf16[72,2048]{1,0:T(8,128)(2,1)S(1)}, u32[]{:S(2)}, u32[]{:S(2)}) collective-permute-start(bf16[72,2048]{1,0:T(8,128)(2,1)S(1)} %collective-permute-done.1.refs_2_), channel_id=1, source_target_pairs={{0,16},{16,0},{32,48},{48,32},{64,80},{80,64},{96,112},{112,96},{1... | collective-permute-start | bytes 884744 | tf_op jit(solution)/shard_map/ppermute | solution.py:318
  51.9 3.5 %collective-permute-start.4 = (bf16[72,2048]{1,0:T(8,128)(2,1)S(1)}, bf16[72,2048]{1,0:T(8,128)(2,1)S(1)}, u32[]{:S(2)}, u32[]{:S(2)}) collective-permute-start(bf16[72,2048]{1,0:T(8,128)(2,1)S(1)} %collective-permute-done.refs_1_), channel_id=1, source_target_pairs={{0,16},{16,0},{32,48},{48,32},{64,80},{80,64},{96,112},{112,96},{1... | collective-permute-start | bytes 884744 | tf_op jit(solution)/shard_map/ppermute | solution.py:318
  55.5 28.7 %copy-start.1 = (s32[127]{0:T(128)S(1)}, s32[127]{0:T(128)}, u32[]{:S(2)}) copy-start(s32[127]{0:T(128)} %param.9) | copy-start | bytes 1528
  55.5 28.7 %copy-start.2 = (s32[127]{0:T(128)S(1)}, s32[127]{0:T(128)}, u32[]{:S(2)}) copy-start(s32[127]{0:T(128)} %param.10) | copy-start | bytes 1528

commit v3 on v2

--- a/solution.py
+++ b/solution.py
@@ -17,6 +17,7 @@
 FULL = 3
 LEFT = LANES // SUBS
 NEG = -1e30
+CHUNKS = 4
 F32 = jnp.float32
 BF16 = jnp.bfloat16
 MIB = 1 << 20
@@ -131,21 +132,53 @@
     )(*acts)
 
 
-def score_kernel(a_ref, w_ref, out_ref, w_buf, l_buf):
-    depth = (w_ref.shape[1] - 8) // FULL
+def score_kernel(a_ref, w_ref, out_ref, w_buf, t_buf, r_buf, l_buf, sems):
+    depth = w_buf.shape[1]
     groups = depth // 8
     copies = out_ref.shape[0]
     me = lax.axis_index("cells")
     sub = me % SUBS
     start = lax.axis_index("vocab") * (SUBS * (FULL * LANES + LEFT))
-    for i in range(PLANE):
-        rows = slice(i * depth, (i + 1) * depth)
-        for k in range(FULL):
-            w_buf[rows, k * LANES : (k + 1) * LANES] = w_ref[i, k * depth : (k + 1) * depth, :]
-        left = w_ref[i, FULL * depth :, :].astype(F32)
-        pieces = [left] + [pltpu.roll(left, LANES - LEFT * a, 1) for a in range(1, groups)]
-        w_buf[rows, FULL * LANES :] = jnp.concatenate(pieces, axis=0).astype(BF16)
-    l_buf[...] = jnp.dot(a_ref[...], w_buf[...], preferred_element_type=F32)
+    per = PLANE // CHUNKS
+    moves = []
+    for c in range(CHUNKS):
+        blocks = pl.ds(c * per, per)
+        pairs = [
+            (
+                w_ref.at[blocks, pl.ds(k * depth, depth), :],
+                w_buf.at[blocks, :, pl.ds(k * LANES, LANES)],
+            )
+            for k in range(FULL)
+        ]
+        pairs.append((w_ref.at[blocks, pl.ds(FULL * depth, 8), :], t_buf.at[blocks]))
+        moves.append(
+            [
+                pltpu.make_async_copy(source, target, sems.at[c * (FULL + 1) + k])
+                for k, (source, target) in enumerate(pairs)
+            ]
+        )
+    for move in moves:
+        for copy in move:
+            copy.start()
+    for c in range(CHUNKS):
+        for copy in moves[c]:
+            copy.wait()
+        blocks = slice(c * per, (c + 1) * per)
+        for i in range(c * per, (c + 1) * per):
+            left = t_buf[i].astype(F32)
+            pieces = [left] + [pltpu.roll(left, LANES - LEFT * a, 1) for a in range(1, groups)]
+            r_buf[i] = jnp.concatenate(pieces, axis=0).astype(BF16)
+        features = per * depth
+        columns = jnp.concatenate(
+            [
+                w_buf[blocks].reshape(features, FULL * LANES),
+                r_buf[blocks].reshape(features, LANES),
+            ],
+            axis=1,
+        )
+        rows = a_ref[:, c * features : (c + 1) * features]
+        part = jnp.dot(rows, columns, preferred_element_type=F32)
+        l_buf[...] = part if c == 0 else l_buf[...] + part
 
     width = (FULL + 1) * LANES
     lane = lanes_of((1, width))
@@ -155,6 +188,8 @@
         start + sub * (FULL * LANES) + lane,
         start + SUBS * FULL * LANES + sub * LEFT + lane - FULL * LANES,
     ).astype(F32)
+    clean_line = jnp.zeros((1, LANES), F32)
+    slot = lanes_of((1, LANES))
     for t in range(YS):
         parts = []
         for d in range(CORES):
@@ -178,26 +213,31 @@
                     max_patch + jnp.log(sum_patch),
                     cross,
                     jnp.sum(picked, axis=-1, keepdims=True),
-                    jnp.broadcast_to(clean_lse, (KEYS, 1)),
                 )
             )
-        for k in range(4):
+            clean_line = jnp.where(slot == t * CORES + d, clean_lse, clean_line)
+        for k in range(3):
             both = jnp.concatenate([parts[0][k], parts[1][k]], axis=0)
             line = as_line(both)
             for i in range(copies):
-                out_ref[i, 4 * k + t : 4 * k + t + 1, :] = line
+                out_ref[i, :, (4 * k + t) * LANES : (4 * k + t + 1) * LANES] = line
+    for i in range(copies):
+        out_ref[i, :, 12 * LANES :] = clean_line
 
 
 def scored(rows, weights, copies):
     depth = (weights.shape[1] - 8) // FULL
     return pl.pallas_call(
         score_kernel,
-        out_shape=jax.ShapeDtypeStruct((copies, 16, LANES), F32),
-        in_specs=[VMEM, VMEM],
+        out_shape=jax.ShapeDtypeStruct((copies, 1, 13 * LANES), F32),
+        in_specs=[VMEM, pl.BlockSpec(memory_space=pltpu.HBM)],
         out_specs=VMEM,
         scratch_shapes=[
-            pltpu.VMEM((PLANE * depth, (FULL + 1) * LANES), BF16),
+            pltpu.VMEM((PLANE, depth, FULL * LANES), BF16),
+            pltpu.VMEM((PLANE, 8, LANES), BF16),
+            pltpu.VMEM((PLANE, depth, LANES), BF16),
             pltpu.VMEM((2 * YS * ROWS, (FULL + 1) * LANES), F32),
+            pltpu.SemaphoreType.DMA((CHUNKS * (FULL + 1),)),
         ],
         compiler_params=pltpu.CompilerParams(vmem_limit_bytes=12 * MIB),
         name="score",
@@ -205,36 +245,47 @@
 
 
 def merged(lse, cross, answer, clean_lse):
-    top = jnp.max(lse, axis=0)
-    lse = top + jnp.log(jnp.sum(jnp.exp(lse - top), axis=0))
-    top = jnp.max(clean_lse, axis=0)
+    top = jnp.max(lse, axis=0, keepdims=True)
+    lse = top + jnp.log(jnp.sum(jnp.exp(lse - top), axis=0, keepdims=True))
+    top = jnp.max(clean_lse, axis=0, keepdims=True)
     weight = jnp.exp(clean_lse - top)
-    total = jnp.sum(weight, axis=0)
-    cross = jnp.sum(weight * cross, axis=0) / total
-    return lse, cross, jnp.sum(answer, axis=0), top + jnp.log(total)
+    total = jnp.sum(weight, axis=0, keepdims=True)
+    cross = jnp.sum(weight * cross, axis=0, keepdims=True) / total
+    return lse, cross, jnp.sum(answer, axis=0, keepdims=True), top + jnp.log(total)
 
 
 def merge_kernel(in_ref, layer_ref, pos_ref, out_ref, *, position_count):
     me = lax.axis_index("cells")
     y, core = (me // CORES) % YS, me % CORES
-    lines = []
-    for value in merged(*(in_ref[:, 4 * k : 4 * k + 4, :] for k in range(4))):
-        value = jnp.where(core == 1, pltpu.roll(value, KEYS, 1), value)
-        placed = value
-        for shift in range(1, YS):
-            turned = jnp.concatenate([value[YS - shift :], value[: YS - shift]], axis=0)
-            placed = jnp.where(y == shift, turned, placed)
-        lines.append(placed)
+    lane = lanes_of((1, LANES))
+    clean = in_ref[:, 0, 12 * LANES :]
+    by_slot = []
+    for t in range(YS):
+        first, second = (clean[:, t * CORES + d : t * CORES + d + 1] for d in range(CORES))
+        clean_lse = jnp.where(lane < KEYS, first, second)
+        stats = merged(
+            *(in_ref[:, 0, (4 * k + t) * LANES : (4 * k + t + 1) * LANES] for k in range(3)),
+            clean_lse,
+        )
+        by_slot.append(
+            [jnp.where(core == 1, pltpu.roll(value, KEYS, 1), value) for value in stats]
+        )
     hits = key_hits(layer_ref, pos_ref, position_count)
     count = as_line(jnp.sum(hits, axis=1, keepdims=True))
-    lane = lanes_of((YS, LANES))
-    row = lax.broadcasted_iota(jnp.int32, (YS, LANES), 0)
     half = KEYS // 2
-    count = jnp.where(row == 0, pltpu.roll(count, half, 1), count)
-    lines[3] = jnp.where((lane // half == 1) & (row < 2), count, lines[3])
+    lines = []
+    for k in range(4):
+        for t in range(YS):
+            line = by_slot[t][k]
+            for shift in range(1, YS):
+                line = jnp.where(y == shift, by_slot[(t - shift) % YS][k], line)
+            if k == 3 and t < 2:
+                piece = pltpu.roll(count, half, 1) if t == 0 else count
+                line = jnp.where(lane // half == 1, piece, line)
+            lines.append(line)
+    block = jnp.concatenate(lines, axis=0)
     for i in range(out_ref.shape[0]):
-        for k in range(4):
-            out_ref[i, 4 * k : 4 * k + 4, :] = lines[k]
+        out_ref[i] = block
 
 
 def merged_over_vocab(pieces, layer, pos, position_count):
@@ -265,9 +316,12 @@
             jnp.where(lane % KEYS < half, clean[s], pltpu.roll(clean[s], half, 1))[None]
             for s in range(SUBS)
         ]
-        lse, cross, answer, clean_lse = merged(
-            *(in_ref[group, 4 * k : 4 * k + 4, :] for k in range(3)),
-            jnp.concatenate(spread, axis=0),
+        lse, cross, answer, clean_lse = (
+            value[0]
+            for value in merged(
+                *(in_ref[group, 4 * k : 4 * k + 4, :] for k in range(3)),
+                jnp.concatenate(spread, axis=0),
+            )
         )
         divergence = cross - clean_lse + lse
         for s in range(SUBS):

time: 102 us -> 101 us (level)
  no operation moved by 1% of the time
where the time goes in v3:
time: 101 us
  blocking collectives  39.7 us (39%)
  starting transfers between devices  33 us (33%)
  waiting for transfers between devices  18.4 us (18%)
  Pallas kernels  8.29 us (8%)
  between operations  1.44 us (1%)
    all_to_all x1, blocking collectives, on_device(): stats = lax.all_to_all(stats, 'vocab', 0, 0, tiled=True)  24.1 us
    ppermute x7, starting transfers between devices, moved(): return lax.ppermute(value, 'cells', [(i, to(i)) for i in range(PLANE)])  21.7 us
    ppermute x7, waiting for transfers between devices, moved(): return lax.ppermute(value, 'cells', [(i, to(i)) for i in range(PLANE)])  18.4 us
    all_to_all x1, blocking collectives, on_device(): pieces = lax.all_to_all(pieces, 'cells', 0, 0, tiled=True)  15.6 us
    all_to_all x1, starting transfers between devices, on_device(): weights = lax.all_to_all(sent, 'cells', 0, 0, tiled=True)  11.3 us
    pallas_call x1, Pallas kernels, scored(): pl.pallas_call(score_kernel, out_shape=jax.ShapeDtypeStruct((copies, 1, 1...  4.27 us
    pallas_call x1, Pallas kernels, prepared(): pl.pallas_call(prepare_kernel, out_shape=(jax.ShapeDtypeStruct((ROWS, cle...  2.56 us
  transfers between devices with their start and end apart: 8, of which 3 were waited for; matrix products, arithmetic and copies ran while one was open for 0% of the time, Pallas kernels for 0%

profile of v3, /device:TPU:1, one launch (start us, length us, event | category | flops | bytes accessed | tf_op | source)
XLA Modules:
  0.0 100.9 jit_solution(2760003162791229443)
XLA Ops:
  1.3 2.6 %prepare.1 = (bf16[72,2048]{1,0:T(8,128)(2,1)}, bf16[32,200,128]{2,1,0:T(8,128)(2,1)}) custom-call(s32[1]{0:T(128)S(6)} %copy.10.answer_ref, f32[1,2048]{1,0:T(1,128)} %refs_0_.1, bf16[64,2048]{1,0:T(8,128)(2,1)} %bitcast.9, f32[1,2048]{1,0:T(1,128)} %bitcast.10, bf16[64,3200]{1,0:T(8,128)(2,1)} %refs_3_.1), custom_call_target="tpu_custom_call" | custom-call | tf_op jit(solution)/shard_map/prepare/pallas_call | solution.py:103
  3.9 11.3 %all-to-all-start = ((bf16[32,200,128]{2,1,0:T(8,128)(2,1)}), bf16[32,200,128]{2,1,0:T(8,128)(2,1)}, u32[]{:S(2)}, u32[]{:S(2)}) async-start(bf16[32,200,128]{2,1,0:T(8,128)(2,1)} %get-tuple-element.9), calls=%async_computation | async-start | bytes 3276800 | tf_op jit(solution)/shard_map/all_to_all | solution.py:396
  15.2 3.3 %collective-permute-start.2 = (bf16[72,2048]{1,0:T(8,128)(2,1)S(1)}, bf16[72,2048]{1,0:T(8,128)(2,1)S(1)}, u32[]{:S(2)}, u32[]{:S(2)}) collective-permute-start(bf16[72,2048]{1,0:T(8,128)(2,1)S(1)} %copy-done), channel_id=1, source_target_pairs={{0,32},{16,48},{32,64},{48,80},{64,96},{80,112},{96,0},{112,16},{1... | collective-permute-start | bytes 884744 | tf_op jit(solution)/shard_map/ppermute | solution.py:372
  18.4 4.3 %collective-permute-start.1 = (bf16[72,2048]{1,0:T(8,128)(2,1)S(1)}, bf16[72,2048]{1,0:T(8,128)(2,1)S(1)}, u32[]{:S(2)}, u32[]{:S(2)}) collective-permute-start(bf16[72,2048]{1,0:T(8,128)(2,1)S(1)} %copy-done), channel_id=1, source_target_pairs={{0,64},{16,80},{32,96},{48,112},{64,0},{80,16},{96,32},{112,48},{1... | collective-permute-start | bytes 884744 | tf_op jit(solution)/shard_map/ppermute | solution.py:372
  22.8 3.1 %collective-permute-start = (bf16[72,2048]{1,0:T(8,128)(2,1)S(1)}, bf16[72,2048]{1,0:T(8,128)(2,1)S(1)}, u32[]{:S(2)}, u32[]{:S(2)}) collective-permute-start(bf16[72,2048]{1,0:T(8,128)(2,1)S(1)} %copy-done), channel_id=1, source_target_pairs={{0,96},{16,112},{32,0},{48,16},{64,32},{80,48},{96,64},{112,80},{1... | collective-permute-start | bytes 884744 | tf_op jit(solution)/shard_map/ppermute | solution.py:372
  25.9 3.1 %collective-permute-start.3 = (bf16[72,2048]{1,0:T(8,128)(2,1)S(1)}, bf16[72,2048]{1,0:T(8,128)(2,1)S(1)}, u32[]{:S(2)}, u32[]{:S(2)}) collective-permute-start(bf16[72,2048]{1,0:T(8,128)(2,1)S(1)} %copy-done), channel_id=1, source_target_pairs={{0,16},{16,0},{32,48},{48,32},{64,80},{80,64},{96,112},{112,96},{1... | collective-permute-start | bytes 884744 | tf_op jit(solution)/shard_map/ppermute | solution.py:372
  29.0 13.4 %collective-permute-done.2.refs_3_ = bf16[72,2048]{1,0:T(8,128)(2,1)S(1)} collective-permute-done((bf16[72,2048]{1,0:T(8,128)(2,1)S(1)}, bf16[72,2048]{1,0:T(8,128)(2,1)S(1)}, u32[]{:S(2)}, u32[]{:S(2)}) %collective-permute-start.2) | collective-permute-done | bytes 294944 | tf_op jit(solution)/shard_map/ppermute | solution.py:372
  42.4 3.1 %collective-permute-start.6 = (bf16[72,2048]{1,0:T(8,128)(2,1)S(1)}, bf16[72,2048]{1,0:T(8,128)(2,1)S(1)}, u32[]{:S(2)}, u32[]{:S(2)}) collective-permute-start(bf16[72,2048]{1,0:T(8,128)(2,1)S(1)} %collective-permute-done.2.refs_3_), channel_id=1, source_target_pairs={{0,16},{16,0},{32,48},{48,32},{64,80},{80,64},{96,112},{112,96},{1... | collective-permute-start | bytes 884744 | tf_op jit(solution)/shard_map/ppermute | solution.py:372
  45.5 3.5 %collective-permute-done.1.refs_2_ = bf16[72,2048]{1,0:T(8,128)(2,1)S(1)} collective-permute-done((bf16[72,2048]{1,0:T(8,128)(2,1)S(1)}, bf16[72,2048]{1,0:T(8,128)(2,1)S(1)}, u32[]{:S(2)}, u32[]{:S(2)}) %collective-permute-start.1) | collective-permute-done | bytes 294944 | tf_op jit(solution)/shard_map/ppermute | solution.py:372
  49.0 2.9 %collective-permute-start.5 = (bf16[72,2048]{1,0:T(8,128)(2,1)S(1)}, bf16[72,2048]{1,0:T(8,128)(2,1)S(1)}, u32[]{:S(2)}, u32[]{:S(2)}) collective-permute-start(bf16[72,2048]{1,0:T(8,128)(2,1)S(1)} %collective-permute-done.1.refs_2_), channel_id=1, source_target_pairs={{0,16},{16,0},{32,48},{48,32},{64,80},{80,64},{96,112},{112,96},{1... | collective-permute-start | bytes 884744 | tf_op jit(solution)/shard_map/ppermute | solution.py:372
  51.9 0.0 collective-permute-done.refs_1_
  51.9 1.9 %collective-permute-start.4 = (bf16[72,2048]{1,0:T(8,128)(2,1)S(1)}, bf16[72,2048]{1,0:T(8,128)(2,1)S(1)}, u32[]{:S(2)}, u32[]{:S(2)}) collective-permute-start(bf16[72,2048]{1,0:T(8,128)(2,1)S(1)} %collective-permute-done.refs_1_), channel_id=1, source_target_pairs={{0,16},{16,0},{32,48},{48,32},{64,80},{80,64},{96,112},{112,96},{1... | collective-permute-start | bytes 884744 | tf_op jit(solution)/shard_map/ppermute | solution.py:372
  53.8 0.0 collective-permute-done.3.refs_4_
  53.8 0.0 collective-permute-done.6.refs_7_
  53.8 0.0 collective-permute-done.5.refs_6_
  53.8 1.5 %collective-permute-done.4.refs_5_ = bf16[72,2048]{1,0:T(8,128)(2,1)S(1)} collective-permute-done((bf16[72,2048]{1,0:T(8,128)(2,1)S(1)}, bf16[72,2048]{1,0:T(8,128)(2,1)S(1)}, u32[]{:S(2)}, u32[]{:S(2)}) %collective-permute-start.4) | collective-permute-done | bytes 294944 | tf_op jit(solution)/shard_map/ppermute | solution.py:372
  55.4 0.2 stack.1.a_ref
  55.5 0.0 copy-start.1
  55.5 0.0 copy-start.2
  55.5 4.3 %score.1 = f32[16,1,1664]{2,1,0:T(1,128)S(1)} custom-call(bf16[576,2048]{1,0:T(8,128)(2,1)S(1)} %stack.1.a_ref, bf16[32,200,128]{2,1,0:T(8,128)(2,1)} %all-to-all-done.w_ref), custom_call_target="tpu_custom_call" | custom-call | tf_op jit(solution)/shard_map/score/pallas_call | solution.py:230
  59.8 24.1 %all_to_all.15.in_ref = f32[16,1,1664]{2,1,0:T(1,128)S(1)} all-to-all(f32[16,1,1664]{2,1,0:T(1,128)S(1)} %score.1), channel_id=1, replica_groups=mesh['cells'=32,'vocab'=16] {'vocab'}, dimensions={0} | all-to-all | bytes 212992 | tf_op jit(solution)/shard_map/all_to_all | solution.py:401
  83.9 0.4 merge.1
  84.4 15.6 %all_to_all.16.in_ref = f32[32,16,128]{2,1,0:T(8,128)S(1)} all-to-all(f32[32,16,128]{2,1,0:T(8,128)S(1)} %merge.1), channel_id=1, replica_groups=mesh['cells'=32,'vocab'=16] {'cells'}, dimensions={0} | all-to-all | bytes 524288 | tf_op jit(solution)/shard_map/all_to_all | solution.py:404
  100.0 0.9 finish.1
  (5 shorter events, 0.0 us)
Async XLA Ops:
  3.8 11.3 %copy-start = (bf16[72,2048]{1,0:T(8,128)(2,1)S(1)}, bf16[72,2048]{1,0:T(8,128)(2,1)}, u32[]{:S(2)}) copy-start(bf16[72,2048]{1,0:T(8,128)(2,1)} %get-tuple-element.8.refs_0_) | copy-start | bytes 884740
  3.9 51.7 %all-to-all-start = ((bf16[32,200,128]{2,1,0:T(8,128)(2,1)}), bf16[32,200,128]{2,1,0:T(8,128)(2,1)}, u32[]{:S(2)}, u32[]{:S(2)}) async-start(bf16[32,200,128]{2,1,0:T(8,128)(2,1)} %get-tuple-element.9), calls=%async_computation | async-start | bytes 3276800 | tf_op jit(solution)/shard_map/all_to_all | solution.py:396
  15.2 27.2 %collective-permute-start.2 = (bf16[72,2048]{1,0:T(8,128)(2,1)S(1)}, bf16[72,2048]{1,0:T(8,128)(2,1)S(1)}, u32[]{:S(2)}, u32[]{:S(2)}) collective-permute-start(bf16[72,2048]{1,0:T(8,128)(2,1)S(1)} %copy-done), channel_id=1, source_target_pairs={{0,32},{16,48},{32,64},{48,80},{64,96},{80,112},{96,0},{112,16},{1... | collective-permute-start | bytes 884744 | tf_op jit(solution)/shard_map/ppermute | solution.py:372
  18.4 30.6 %collective-permute-start.1 = (bf16[72,2048]{1,0:T(8,128)(2,1)S(1)}, bf16[72,2048]{1,0:T(8,128)(2,1)S(1)}, u32[]{:S(2)}, u32[]{:S(2)}) collective-permute-start(bf16[72,2048]{1,0:T(8,128)(2,1)S(1)} %copy-done), channel_id=1, source_target_pairs={{0,64},{16,80},{32,96},{48,112},{64,0},{80,16},{96,32},{112,48},{1... | collective-permute-start | bytes 884744 | tf_op jit(solution)/shard_map/ppermute | solution.py:372
  22.8 29.1 %collective-permute-start = (bf16[72,2048]{1,0:T(8,128)(2,1)S(1)}, bf16[72,2048]{1,0:T(8,128)(2,1)S(1)}, u32[]{:S(2)}, u32[]{:S(2)}) collective-permute-start(bf16[72,2048]{1,0:T(8,128)(2,1)S(1)} %copy-done), channel_id=1, source_target_pairs={{0,96},{16,112},{32,0},{48,16},{64,32},{80,48},{96,64},{112,80},{1... | collective-permute-start | bytes 884744 | tf_op jit(solution)/shard_map/ppermute | solution.py:372
  25.9 27.9 %collective-permute-start.3 = (bf16[72,2048]{1,0:T(8,128)(2,1)S(1)}, bf16[72,2048]{1,0:T(8,128)(2,1)S(1)}, u32[]{:S(2)}, u32[]{:S(2)}) collective-permute-start(bf16[72,2048]{1,0:T(8,128)(2,1)S(1)} %copy-done), channel_id=1, source_target_pairs={{0,16},{16,0},{32,48},{48,32},{64,80},{80,64},{96,112},{112,96},{1... | collective-permute-start | bytes 884744 | tf_op jit(solution)/shard_map/ppermute | solution.py:372
  42.4 11.5 %collective-permute-start.6 = (bf16[72,2048]{1,0:T(8,128)(2,1)S(1)}, bf16[72,2048]{1,0:T(8,128)(2,1)S(1)}, u32[]{:S(2)}, u32[]{:S(2)}) collective-permute-start(bf16[72,2048]{1,0:T(8,128)(2,1)S(1)} %collective-permute-done.2.refs_3_), channel_id=1, source_target_pairs={{0,16},{16,0},{32,48},{48,32},{64,80},{80,64},{96,112},{112,96},{1... | collective-permute-start | bytes 884744 | tf_op jit(solution)/shard_map/ppermute | solution.py:372
  49.0 4.8 %collective-permute-start.5 = (bf16[72,2048]{1,0:T(8,128)(2,1)S(1)}, bf16[72,2048]{1,0:T(8,128)(2,1)S(1)}, u32[]{:S(2)}, u32[]{:S(2)}) collective-permute-start(bf16[72,2048]{1,0:T(8,128)(2,1)S(1)} %collective-permute-done.1.refs_2_), channel_id=1, source_target_pairs={{0,16},{16,0},{32,48},{48,32},{64,80},{80,64},{96,112},{112,96},{1... | collective-permute-start | bytes 884744 | tf_op jit(solution)/shard_map/ppermute | solution.py:372
  51.9 3.5 %collective-permute-start.4 = (bf16[72,2048]{1,0:T(8,128)(2,1)S(1)}, bf16[72,2048]{1,0:T(8,128)(2,1)S(1)}, u32[]{:S(2)}, u32[]{:S(2)}) collective-permute-start(bf16[72,2048]{1,0:T(8,128)(2,1)S(1)} %collective-permute-done.refs_1_), channel_id=1, source_target_pairs={{0,16},{16,0},{32,48},{48,32},{64,80},{80,64},{96,112},{112,96},{1... | collective-permute-start | bytes 884744 | tf_op jit(solution)/shard_map/ppermute | solution.py:372
  55.5 28.4 %copy-start.1 = (s32[127]{0:T(128)S(1)}, s32[127]{0:T(128)}, u32[]{:S(2)}) copy-start(s32[127]{0:T(128)} %param.9) | copy-start | bytes 1528
  55.5 28.4 %copy-start.2 = (s32[127]{0:T(128)S(1)}, s32[127]{0:T(128)}, u32[]{:S(2)}) copy-start(s32[127]{0:T(128)} %param.10) | copy-start | bytes 1528

commit v4 on v3

--- a/solution.py
+++ b/solution.py
@@ -13,11 +13,11 @@
 PLANE = XS * SUBS
 LANES = 128
 KEYS = 64
-ROWS = 72
+USED = SUBS * KEYS + 16
 FULL = 3
 LEFT = LANES // SUBS
 NEG = -1e30
-CHUNKS = 4
+CHUNKS = 2
 F32 = jnp.float32
 BF16 = jnp.bfloat16
 MIB = 1 << 20
@@ -69,16 +69,20 @@
         mean_square = jnp.sum(values * values, axis=-1, keepdims=True) * (1.0 / features)
         return values * lax.rsqrt(mean_square + 1e-06) * gain
 
-    act_ref[:KEYS, :] = normed(clean + delta_ref[...].astype(F32)).astype(BF16)
+    tiles = features // LANES
+    patched = normed(clean + delta_ref[...].astype(F32)).astype(BF16)
+    for k in range(tiles):
+        act_ref[k * KEYS : (k + 1) * KEYS, :] = patched[:, k * LANES : (k + 1) * LANES]
     answer = answer_ref[0]
     high = lax.shift_right_logical(answer, 8).astype(F32)
     low = (answer & 255).astype(F32)
-    shape = (ROWS - KEYS, features)
-    row = lax.broadcasted_iota(jnp.int32, shape, 0)
-    lane = lanes_of(shape)
+    clean_row = normed(clean)
+    lines = [clean_row[:, k * LANES : (k + 1) * LANES] for k in range(tiles)]
+    row = lax.broadcasted_iota(jnp.int32, (8, LANES), 0)
+    lane = lanes_of((8, LANES))
     digits = jnp.where(lane == 0, high, jnp.where(lane == 1, low, 0.0))
-    tail = jnp.where(row == 0, normed(clean), jnp.where(row == 1, digits, 0.0))
-    act_ref[KEYS:, :] = tail.astype(BF16)
+    lines.append(jnp.where(row == 0, digits, 0.0))
+    act_ref[tiles * KEYS :, :] = jnp.concatenate(lines, axis=0).astype(BF16)
 
 
 def prepare_kernel(answer_ref, *refs):
@@ -99,11 +103,12 @@
 
 def prepared(answer_ids, clean_resid, delta_table, norm_gain, unembed):
     arrays = (clean_resid, delta_table, norm_gain, unembed)
+    tiles = clean_resid.shape[1] // LANES
     depth = unembed.shape[0]
     return pl.pallas_call(
         prepare_kernel,
         out_shape=(
-            jax.ShapeDtypeStruct((ROWS, clean_resid.shape[1]), BF16),
+            jax.ShapeDtypeStruct((tiles * (KEYS + 1) + 8, LANES), BF16),
             jax.ShapeDtypeStruct((PLANE, FULL * depth + 8, LANES), BF16),
         ),
         in_specs=[SMEM] + [pl.BlockSpec(memory_space=pltpu.HBM)] * 4,
@@ -117,14 +122,26 @@
 
 def stack_kernel(*refs):
     acts, out_ref = refs[:SUBS], refs[SUBS]
+    tiles = out_ref.shape[1] // LANES
     for j in range(SUBS):
-        out_ref[j * ROWS : (j + 1) * ROWS, :] = acts[j][...]
+        for k in range(tiles):
+            out_ref[j * KEYS : (j + 1) * KEYS, k * LANES : (k + 1) * LANES] = acts[j][
+                k * KEYS : (k + 1) * KEYS, :
+            ]
+    tails = [acts[j][tiles * KEYS :, :].astype(F32) for j in range(SUBS)]
+    digits = jnp.concatenate([tail[tiles : tiles + 1] for tail in tails], axis=0)
+    for k in range(tiles):
+        lines = [tail[k : k + 1] for tail in tails]
+        spare = digits if k == 0 else jnp.zeros((SUBS, LANES), F32)
+        block = jnp.concatenate(lines + [spare], axis=0).astype(BF16)
+        out_ref[SUBS * KEYS : USED, k * LANES : (k + 1) * LANES] = block
 
 
 def stacked(acts):
+    tiles = acts[0].shape[0] // (KEYS + 1)
     return pl.pallas_call(
         stack_kernel,
-        out_shape=jax.ShapeDtypeStruct((SUBS * ROWS, acts[0].shape[1]), BF16),
+        out_shape=jax.ShapeDtypeStruct((SUBS * (KEYS + 8), tiles * LANES), BF16),
         in_specs=[VMEM] * SUBS,
         out_specs=VMEM,
         compiler_params=pltpu.CompilerParams(vmem_limit_bytes=8 * MIB),
@@ -176,9 +193,14 @@
             ],
             axis=1,
         )
-        rows = a_ref[:, c * features : (c + 1) * features]
+        rows = a_ref[:USED, c * features : (c + 1) * features]
         part = jnp.dot(rows, columns, preferred_element_type=F32)
-        l_buf[...] = part if c == 0 else l_buf[...] + part
+        part = part if c == 0 else l_buf[...] + part
+        if c < CHUNKS - 1:
+            l_buf[...] = part
+    l_buf[:, : FULL * LANES] = part[:, : FULL * LANES]
+    last = part[:, FULL * LANES :]
+    l_buf[:, FULL * LANES :] = jnp.where(lanes_of(last.shape) < LEFT, last, NEG)
 
     width = (FULL + 1) * LANES
     lane = lanes_of((1, width))
@@ -188,22 +210,22 @@
         start + sub * (FULL * LANES) + lane,
         start + SUBS * FULL * LANES + sub * LEFT + lane - FULL * LANES,
     ).astype(F32)
+    tail = a_ref[SUBS * KEYS : USED, 0:LANES].astype(F32)
     clean_line = jnp.zeros((1, LANES), F32)
     slot = lanes_of((1, LANES))
     for t in range(YS):
         parts = []
         for d in range(CORES):
-            at = (d * YS + t) * ROWS
-            clean = jnp.where(kept, l_buf[at + KEYS : at + KEYS + 1, :], NEG)
+            j = d * YS + t
+            clean = l_buf[SUBS * KEYS + j : SUBS * KEYS + j + 1, :]
             max_clean = jnp.max(clean, axis=-1, keepdims=True)
             weight = jnp.exp(clean - max_clean)
             sum_clean = jnp.sum(weight, axis=-1, keepdims=True)
             weight = weight * (1.0 / sum_clean)
             clean_lse = max_clean + jnp.log(sum_clean)
-            tail = a_ref[at + KEYS : at + ROWS, 0:LANES].astype(F32)
-            digits = tail[1:2]
+            digits = tail[SUBS + j : SUBS + j + 1]
             answer = digits[:, 0:1] * 256.0 + digits[:, 1:2]
-            logits = jnp.where(kept, l_buf[at : at + KEYS, :], NEG)
+            logits = l_buf[j * KEYS : (j + 1) * KEYS, :]
             max_patch = jnp.max(logits, axis=-1, keepdims=True)
             sum_patch = jnp.sum(jnp.exp(logits - max_patch), axis=-1, keepdims=True)
             cross = jnp.sum(weight * (clean - logits), axis=-1, keepdims=True)
@@ -236,7 +258,7 @@
             pltpu.VMEM((PLANE, depth, FULL * LANES), BF16),
             pltpu.VMEM((PLANE, 8, LANES), BF16),
             pltpu.VMEM((PLANE, depth, LANES), BF16),
-            pltpu.VMEM((2 * YS * ROWS, (FULL + 1) * LANES), F32),
+            pltpu.VMEM((USED, (FULL + 1) * LANES), F32),
             pltpu.SemaphoreType.DMA((CHUNKS * (FULL + 1),)),
         ],
         compiler_params=pltpu.CompilerParams(vmem_limit_bytes=12 * MIB),

time: 101 us -> 100 us (0.990)
  waiting for transfers between devices: 18.4 us -> 17.2 us
    ppermute x7, waiting for transfers between devices: 18.4 us -> 17.2 us  [moved(): return lax.ppermute(value, 'cells', [(i, to(i)) for i in range(PLANE)])]
where the time goes in v4:
time: 100 us; the launch traced here: 99.7 us
  blocking collectives  39.7 us (40%)
  starting transfers between devices  33 us (33%)
  waiting for transfers between devices  17.2 us (17%)
  Pallas kernels  8.33 us (8%)
  between operations  1.45 us (1%)
    all_to_all x1, blocking collectives, on_device(): stats = lax.all_to_all(stats, 'vocab', 0, 0, tiled=True)  24.1 us
    ppermute x7, starting transfers between devices, moved(): return lax.ppermute(value, 'cells', [(i, to(i)) for i in range(PLANE)])  21.7 us
    ppermute x7, waiting for transfers between devices, moved(): return lax.ppermute(value, 'cells', [(i, to(i)) for i in range(PLANE)])  17.2 us
    all_to_all x1, blocking collectives, on_device(): pieces = lax.all_to_all(pieces, 'cells', 0, 0, tiled=True)  15.6 us
    all_to_all x1, starting transfers between devices, on_device(): weights = lax.all_to_all(sent, 'cells', 0, 0, tiled=True)  11.3 us
    pallas_call x1, Pallas kernels, scored(): pl.pallas_call(score_kernel, out_shape=jax.ShapeDtypeStruct((copies, 1, 1...  4.03 us
    pallas_call x1, Pallas kernels, prepared(): pl.pallas_call(prepare_kernel, out_shape=(jax.ShapeDtypeStruct((tiles * (...  2.56 us
  transfers between devices with their start and end apart: 8, of which 3 were waited for; matrix products, arithmetic and copies ran while one was open for 0% of the time, Pallas kernels for 0%

profile of v4, /device:TPU:1, one launch (start us, length us, event | category | flops | bytes accessed | tf_op | source)
XLA Modules:
  0.0 99.7 jit_solution(7582370620748485762)
XLA Ops:
  1.3 2.6 %prepare.1 = (bf16[1048,128]{1,0:T(8,128)(2,1)}, bf16[32,200,128]{2,1,0:T(8,128)(2,1)}) custom-call(s32[1]{0:T(128)S(6)} %copy.10.answer_ref, f32[1,2048]{1,0:T(1,128)} %refs_0_.1, bf16[64,2048]{1,0:T(8,128)(2,1)} %bitcast.9, f32[1,2048]{1,0:T(1,128)} %bitcast.10, bf16[64,3200]{1,0:T(8,128)(2,1)} %refs_3_.1), custom_call_target="tpu_custom_call" | custom-call | tf_op jit(solution)/shard_map/prepare/pallas_call | solution.py:108
  3.9 11.3 %all-to-all-start = ((bf16[32,200,128]{2,1,0:T(8,128)(2,1)}), bf16[32,200,128]{2,1,0:T(8,128)(2,1)}, u32[]{:S(2)}, u32[]{:S(2)}) async-start(bf16[32,200,128]{2,1,0:T(8,128)(2,1)} %get-tuple-element.9), calls=%async_computation | async-start | bytes 3276800 | tf_op jit(solution)/shard_map/all_to_all | solution.py:418
  15.2 3.3 %collective-permute-start.2 = (bf16[1048,128]{1,0:T(8,128)(2,1)S(1)}, bf16[1048,128]{1,0:T(8,128)(2,1)S(1)}, u32[]{:S(2)}, u32[]{:S(2)}) collective-permute-start(bf16[1048,128]{1,0:T(8,128)(2,1)S(1)} %copy-done), channel_id=1, source_target_pairs={{0,32},{16,48},{32,64},{48,80},{64,96},{80,112},{96,0},{112,16},{1... | collective-permute-start | bytes 804872 | tf_op jit(solution)/shard_map/ppermute | solution.py:394
  18.4 4.3 %collective-permute-start.1 = (bf16[1048,128]{1,0:T(8,128)(2,1)S(1)}, bf16[1048,128]{1,0:T(8,128)(2,1)S(1)}, u32[]{:S(2)}, u32[]{:S(2)}) collective-permute-start(bf16[1048,128]{1,0:T(8,128)(2,1)S(1)} %copy-done), channel_id=1, source_target_pairs={{0,64},{16,80},{32,96},{48,112},{64,0},{80,16},{96,32},{112,48},{1... | collective-permute-start | bytes 804872 | tf_op jit(solution)/shard_map/ppermute | solution.py:394
  22.8 3.1 %collective-permute-start = (bf16[1048,128]{1,0:T(8,128)(2,1)S(1)}, bf16[1048,128]{1,0:T(8,128)(2,1)S(1)}, u32[]{:S(2)}, u32[]{:S(2)}) collective-permute-start(bf16[1048,128]{1,0:T(8,128)(2,1)S(1)} %copy-done), channel_id=1, source_target_pairs={{0,96},{16,112},{32,0},{48,16},{64,32},{80,48},{96,64},{112,80},{1... | collective-permute-start | bytes 804872 | tf_op jit(solution)/shard_map/ppermute | solution.py:394
  25.9 3.1 %collective-permute-start.3 = (bf16[1048,128]{1,0:T(8,128)(2,1)S(1)}, bf16[1048,128]{1,0:T(8,128)(2,1)S(1)}, u32[]{:S(2)}, u32[]{:S(2)}) collective-permute-start(bf16[1048,128]{1,0:T(8,128)(2,1)S(1)} %copy-done), channel_id=1, source_target_pairs={{0,16},{16,0},{32,48},{48,32},{64,80},{80,64},{96,112},{112,96},{1... | collective-permute-start | bytes 804872 | tf_op jit(solution)/shard_map/ppermute | solution.py:394
  29.0 12.8 %collective-permute-done.2.refs_3_ = bf16[1048,128]{1,0:T(8,128)(2,1)S(1)} collective-permute-done((bf16[1048,128]{1,0:T(8,128)(2,1)S(1)}, bf16[1048,128]{1,0:T(8,128)(2,1)S(1)}, u32[]{:S(2)}, u32[]{:S(2)}) %collective-permute-start.2) | collective-permute-done | bytes 268320 | tf_op jit(solution)/shard_map/ppermute | solution.py:394
  41.8 3.1 %collective-permute-start.6 = (bf16[1048,128]{1,0:T(8,128)(2,1)S(1)}, bf16[1048,128]{1,0:T(8,128)(2,1)S(1)}, u32[]{:S(2)}, u32[]{:S(2)}) collective-permute-start(bf16[1048,128]{1,0:T(8,128)(2,1)S(1)} %collective-permute-done.2.refs_3_), channel_id=1, source_target_pairs={{0,16},{16,0},{32,48},{48,32},{64,80},{80,64},{96,112},{112,96},{1... | collective-permute-start | bytes 804872 | tf_op jit(solution)/shard_map/ppermute | solution.py:394
  44.9 3.0 %collective-permute-done.1.refs_2_ = bf16[1048,128]{1,0:T(8,128)(2,1)S(1)} collective-permute-done((bf16[1048,128]{1,0:T(8,128)(2,1)S(1)}, bf16[1048,128]{1,0:T(8,128)(2,1)S(1)}, u32[]{:S(2)}, u32[]{:S(2)}) %collective-permute-start.1) | collective-permute-done | bytes 268320 | tf_op jit(solution)/shard_map/ppermute | solution.py:394
  47.9 2.9 %collective-permute-start.5 = (bf16[1048,128]{1,0:T(8,128)(2,1)S(1)}, bf16[1048,128]{1,0:T(8,128)(2,1)S(1)}, u32[]{:S(2)}, u32[]{:S(2)}) collective-permute-start(bf16[1048,128]{1,0:T(8,128)(2,1)S(1)} %collective-permute-done.1.refs_2_), channel_id=1, source_target_pairs={{0,16},{16,0},{32,48},{48,32},{64,80},{80,64},{96,112},{112,96},{1... | collective-permute-start | bytes 804872 | tf_op jit(solution)/shard_map/ppermute | solution.py:394
  50.7 0.0 collective-permute-done.refs_1_
  50.7 1.9 %collective-permute-start.4 = (bf16[1048,128]{1,0:T(8,128)(2,1)S(1)}, bf16[1048,128]{1,0:T(8,128)(2,1)S(1)}, u32[]{:S(2)}, u32[]{:S(2)}) collective-permute-start(bf16[1048,128]{1,0:T(8,128)(2,1)S(1)} %collective-permute-done.refs_1_), channel_id=1, source_target_pairs={{0,16},{16,0},{32,48},{48,32},{64,80},{80,64},{96,112},{112,96},{1... | collective-permute-start | bytes 804872 | tf_op jit(solution)/shard_map/ppermute | solution.py:394
  52.7 0.0 collective-permute-done.3.refs_4_
  52.7 0.0 collective-permute-done.6.refs_7_
  52.7 0.0 collective-permute-done.5.refs_6_
  52.7 1.5 %collective-permute-done.4.refs_5_ = bf16[1048,128]{1,0:T(8,128)(2,1)S(1)} collective-permute-done((bf16[1048,128]{1,0:T(8,128)(2,1)S(1)}, bf16[1048,128]{1,0:T(8,128)(2,1)S(1)}, u32[]{:S(2)}, u32[]{:S(2)}) %collective-permute-start.4) | collective-permute-done | bytes 268320 | tf_op jit(solution)/shard_map/ppermute | solution.py:394
  54.2 0.4 stack.1.a_ref
  54.6 0.0 copy-start.1
  54.6 0.0 copy-start.2
  54.6 4.0 %score.1 = f32[16,1,1664]{2,1,0:T(1,128)S(1)} custom-call(bf16[576,2048]{1,0:T(8,128)(2,1)S(1)} %stack.1.a_ref, bf16[32,200,128]{2,1,0:T(8,128)(2,1)} %all-to-all-done.w_ref), custom_call_target="tpu_custom_call" | custom-call | tf_op jit(solution)/shard_map/score/pallas_call | solution.py:252
  58.7 24.1 %all_to_all.15.in_ref = f32[16,1,1664]{2,1,0:T(1,128)S(1)} all-to-all(f32[16,1,1664]{2,1,0:T(1,128)S(1)} %score.1), channel_id=1, replica_groups=mesh['cells'=32,'vocab'=16] {'vocab'}, dimensions={0} | all-to-all | bytes 212992 | tf_op jit(solution)/shard_map/all_to_all | solution.py:423
  82.8 0.4 merge.1
  83.2 15.6 %all_to_all.16.in_ref = f32[32,16,128]{2,1,0:T(8,128)S(1)} all-to-all(f32[32,16,128]{2,1,0:T(8,128)S(1)} %merge.1), channel_id=1, replica_groups=mesh['cells'=32,'vocab'=16] {'cells'}, dimensions={0} | all-to-all | bytes 524288 | tf_op jit(solution)/shard_map/all_to_all | solution.py:426
  98.9 0.9 finish.1
  (5 shorter events, 0.0 us)
Async XLA Ops:
  3.8 11.3 %copy-start = (bf16[1048,128]{1,0:T(8,128)(2,1)S(1)}, bf16[1048,128]{1,0:T(8,128)(2,1)}, u32[]{:S(2)}) copy-start(bf16[1048,128]{1,0:T(8,128)(2,1)} %get-tuple-element.8.refs_0_) | copy-start | bytes 804868
  3.9 50.8 %all-to-all-start = ((bf16[32,200,128]{2,1,0:T(8,128)(2,1)}), bf16[32,200,128]{2,1,0:T(8,128)(2,1)}, u32[]{:S(2)}, u32[]{:S(2)}) async-start(bf16[32,200,128]{2,1,0:T(8,128)(2,1)} %get-tuple-element.9), calls=%async_computation | async-start | bytes 3276800 | tf_op jit(solution)/shard_map/all_to_all | solution.py:418
  15.2 26.6 %collective-permute-start.2 = (bf16[1048,128]{1,0:T(8,128)(2,1)S(1)}, bf16[1048,128]{1,0:T(8,128)(2,1)S(1)}, u32[]{:S(2)}, u32[]{:S(2)}) collective-permute-start(bf16[1048,128]{1,0:T(8,128)(2,1)S(1)} %copy-done), channel_id=1, source_target_pairs={{0,32},{16,48},{32,64},{48,80},{64,96},{80,112},{96,0},{112,16},{1... | collective-permute-start | bytes 804872 | tf_op jit(solution)/shard_map/ppermute | solution.py:394
  18.4 29.4 %collective-permute-start.1 = (bf16[1048,128]{1,0:T(8,128)(2,1)S(1)}, bf16[1048,128]{1,0:T(8,128)(2,1)S(1)}, u32[]{:S(2)}, u32[]{:S(2)}) collective-permute-start(bf16[1048,128]{1,0:T(8,128)(2,1)S(1)} %copy-done), channel_id=1, source_target_pairs={{0,64},{16,80},{32,96},{48,112},{64,0},{80,16},{96,32},{112,48},{1... | collective-permute-start | bytes 804872 | tf_op jit(solution)/shard_map/ppermute | solution.py:394
  22.8 28.0 %collective-permute-start = (bf16[1048,128]{1,0:T(8,128)(2,1)S(1)}, bf16[1048,128]{1,0:T(8,128)(2,1)S(1)}, u32[]{:S(2)}, u32[]{:S(2)}) collective-permute-start(bf16[1048,128]{1,0:T(8,128)(2,1)S(1)} %copy-done), channel_id=1, source_target_pairs={{0,96},{16,112},{32,0},{48,16},{64,32},{80,48},{96,64},{112,80},{1... | collective-permute-start | bytes 804872 | tf_op jit(solution)/shard_map/ppermute | solution.py:394
  25.9 26.8 %collective-permute-start.3 = (bf16[1048,128]{1,0:T(8,128)(2,1)S(1)}, bf16[1048,128]{1,0:T(8,128)(2,1)S(1)}, u32[]{:S(2)}, u32[]{:S(2)}) collective-permute-start(bf16[1048,128]{1,0:T(8,128)(2,1)S(1)} %copy-done), channel_id=1, source_target_pairs={{0,16},{16,0},{32,48},{48,32},{64,80},{80,64},{96,112},{112,96},{1... | collective-permute-start | bytes 804872 | tf_op jit(solution)/shard_map/ppermute | solution.py:394
  41.8 10.9 %collective-permute-start.6 = (bf16[1048,128]{1,0:T(8,128)(2,1)S(1)}, bf16[1048,128]{1,0:T(8,128)(2,1)S(1)}, u32[]{:S(2)}, u32[]{:S(2)}) collective-permute-start(bf16[1048,128]{1,0:T(8,128)(2,1)S(1)} %collective-permute-done.2.refs_3_), channel_id=1, source_target_pairs={{0,16},{16,0},{32,48},{48,32},{64,80},{80,64},{96,112},{112,96},{1... | collective-permute-start | bytes 804872 | tf_op jit(solution)/shard_map/ppermute | solution.py:394
  47.9 4.8 %collective-permute-start.5 = (bf16[1048,128]{1,0:T(8,128)(2,1)S(1)}, bf16[1048,128]{1,0:T(8,128)(2,1)S(1)}, u32[]{:S(2)}, u32[]{:S(2)}) collective-permute-start(bf16[1048,128]{1,0:T(8,128)(2,1)S(1)} %collective-permute-done.1.refs_2_), channel_id=1, source_target_pairs={{0,16},{16,0},{32,48},{48,32},{64,80},{80,64},{96,112},{112,96},{1... | collective-permute-start | bytes 804872 | tf_op jit(solution)/shard_map/ppermute | solution.py:394
  50.7 3.4 %collective-permute-start.4 = (bf16[1048,128]{1,0:T(8,128)(2,1)S(1)}, bf16[1048,128]{1,0:T(8,128)(2,1)S(1)}, u32[]{:S(2)}, u32[]{:S(2)}) collective-permute-start(bf16[1048,128]{1,0:T(8,128)(2,1)S(1)} %collective-permute-done.refs_1_), channel_id=1, source_target_pairs={{0,16},{16,0},{32,48},{48,32},{64,80},{80,64},{96,112},{112,96},{1... | collective-permute-start | bytes 804872 | tf_op jit(solution)/shard_map/ppermute | solution.py:394
  54.6 28.2 %copy-start.1 = (s32[127]{0:T(128)S(1)}, s32[127]{0:T(128)}, u32[]{:S(2)}) copy-start(s32[127]{0:T(128)} %param.9) | copy-start | bytes 1528
  54.6 28.2 %copy-start.2 = (s32[127]{0:T(128)S(1)}, s32[127]{0:T(128)}, u32[]{:S(2)}) copy-start(s32[127]{0:T(128)} %param.10) | copy-start | bytes 1528
